TPU v7x, 256 devices: a whole 4x4x8 slice. The times are simulated.
256 devices in a mesh: gx: 64 (over x, z, core), gy: 4 (over y).
Axes of the slice: x: 4, y: 4, z: 8, core: 2. Of those that a mesh axis runs over, the one named last changes fastest.
Arguments:
- measures: bfloat16 [2097152, 128], P(('gx', 'gy')), may hold values from -6 to 6
- row_keys: int32 [2097152], P(('gx', 'gy')), may hold values from 0 to 131071, as said below
- orders: bfloat16 [131072, 128], P(('gx', 'gy')), may hold values from -6 to 6
- heavy_keys: int32 [512], replicated, may hold values from 0 to 131071, as said below
- key_slot: int32 [131072], replicated, may hold values from 0 to 131071, as said below
Outputs:
- result: bfloat16 [131072, 128], P(('gx', 'gy'))
- heavy_report: bfloat16 [512, 128], P(('gx', 'gy'))
- slot_rows: float32 [131072], P(('gx', 'gy'))
Inputs may be any that keep to these rules, and one draw needn't show every extreme that they name: `heavy_keys`: for each range block d, entries d * 2 to (d + 1) * 2 - 1 are distinct keys of d * 512 to (d + 1) * 512 - 1. `key_slot`: A permutation. Slot s belongs to owner s // 2048 and to quarter (s // 512) % q with q = 4. Key k lies in range block d = k // 512; every range block has exactly 8 keys with slots of each owner, all in quarter d % q. `row_keys`: in the rows of one device, among rows whose key is not heavy, at most 256 have slots of any one owner and at most 64 distinct keys have slots of any one owner; in every device both bounds are reached by some owner.
All inputs are finite; a program needn't handle non-finite values.
Results may differ from a plain program's by a relative error of at most 0.0021.
Values may be sent and summed in bfloat16 or wider, within the bound.
No kernel may reach another device: no remote copies, remote signals or barrier semaphores. Data moves between devices by JAX's collectives and lax.ppermute only.
A program may use at most 64 MiB of HBM per device.

v0:
```python
import math

import jax
import jax.numpy as jnp
from jax import lax
from jax.sharding import PartitionSpec as P


def sent_together(arrays, axis, split_dim, concat_dim, along):
    columns = [a.reshape(*a.shape[:along], -1) for a in arrays]
    both = jnp.concatenate(columns, axis=along)
    out, at, gathered = (
        lax.all_to_all(both, axis, split_axis=split_dim, concat_axis=concat_dim, tiled=True),
        0,
        [],
    )
    for a, column in zip(arrays, columns):
        share = out[..., at : at + column.shape[along]]
        gathered.append(share.reshape(*share.shape[:along], *a.shape[along:]))
        at += column.shape[along]
    return tuple(gathered)


def cut_along(x, dim, length):
    shape = x.shape
    pieces = x.reshape(*shape[:dim], length, shape[dim] // length, *shape[dim + 1 :])
    return jnp.moveaxis(pieces, dim, 0)


def summed_on_arrival(x, axis, dim):
    pieces = cut_along(x, dim, lax.axis_size(axis))
    arrived = lax.all_to_all(pieces, axis, split_axis=0, concat_axis=0, tiled=True)
    return arrived.sum(axis=0)


def side_by_side(arrays, axis, dim, along):
    widths = [math.prod(a.shape[along:]) for a in arrays]
    both = jnp.concatenate(
        [a.reshape(*a.shape[:along], w) for a, w in zip(arrays, widths)], axis=along
    )
    out = summed_on_arrival(both, axis, dim)
    pieces = jnp.split(out, [sum(widths[:k]) for k in range(1, len(widths))], axis=along)
    return tuple((b.reshape(*out.shape[:along], *a.shape[along:]) for a, b in zip(arrays, pieces)))


def block_length():
    return 2048


def one_hot_sums(values, targets, labels, weights):
    block_rows = block_length()
    blocks = targets.shape[0] // block_rows
    columns = values.shape[1]
    span = labels.shape[0]
    exact = values.dtype == jnp.float32

    def add_block(running, block_piece):
        block_values, block_targets, block_weights = block_piece
        matches = block_targets[:, None] == labels[None, :]
        onehot = matches.astype(values.dtype)
        if exact:
            product = lax.dot_general(
                onehot,
                block_values,
                (((0,), (0,)), ((), ())),
                precision=lax.Precision.HIGHEST,
                preferred_element_type=jnp.float32,
            )
        else:
            product = lax.dot_general(
                onehot, block_values, (((0,), (0,)), ((), ())), preferred_element_type=jnp.float32
            )
        totals = running[0] + product
        tallies = running[1] + jnp.sum(matches.astype(jnp.float32) * block_weights[:, None], axis=0)
        return ((totals, tallies), jnp.any(matches, axis=1))

    start_state = (jnp.zeros((span, columns), jnp.float32), jnp.zeros((span,), jnp.float32))
    pieces = (
        values.reshape(blocks, block_rows, columns),
        targets.reshape(blocks, block_rows),
        weights.reshape(blocks, block_rows),
    )
    (totals, tallies), matched = lax.scan(add_block, start_state, pieces)
    return (totals, tallies, matched.reshape(-1))


def body(measures, row_keys, orders, heavy_keys, key_slot):
    row_count, columns = measures.shape
    groups_x = lax.axis_size("gx")
    groups_y = lax.axis_size("gy")
    key_dev = orders.shape[0]
    own_slots = key_dev * groups_y
    heavy_total = heavy_keys.shape[0]
    heavy_each = heavy_total // (groups_x * groups_y)
    capacity = max(row_count // 32, 3 * row_count // (4 * groups_x))
    key_capacity = capacity // 4
    index_x = lax.axis_index("gx")
    index_y = lax.axis_index("gy")
    device = index_x * groups_y + index_y
    unit_rows = jnp.ones((row_count,), jnp.float32)
    heavy_part, heavy_count, heavy_flags = one_hot_sums(measures, row_keys, heavy_keys, unit_rows)
    slot_ids = key_slot[row_keys]
    owner_labels = jnp.arange(groups_x + 1, dtype=jnp.int32)
    own_base = index_x * own_slots
    own_labels = jnp.arange(own_slots, dtype=jnp.int32)
    sort_keys = jnp.where(heavy_flags, groups_x * own_slots, slot_ids)
    ordering = jnp.argsort(sort_keys, stable=True)
    sorted_slots = sort_keys[ordering]
    sorted_owner = sorted_slots // own_slots
    is_light = sorted_owner < groups_x
    fresh = (
        jnp.concatenate([jnp.ones((1,), bool), sorted_slots[1:] != sorted_slots[:-1]]) & is_light
    )
    distinct = jnp.cumsum(fresh.astype(jnp.int32)) - 1
    before = jnp.sum(
        (fresh[:, None] & (sorted_owner[:, None] < owner_labels[None, :])).astype(jnp.int32), axis=0
    )
    segments = groups_x * key_capacity
    segment = jnp.where(
        is_light, sorted_owner * key_capacity + distinct - before[sorted_owner], segments
    )
    row_segment = jnp.zeros((row_count,), jnp.int32).at[ordering].set(segment)
    partial_value, tallies, unused = one_hot_sums(
        measures, row_segment, jnp.arange(segments, dtype=jnp.int32), unit_rows
    )
    sent_slots = jnp.full((segments + 1,), -1, jnp.int32).at[segment].set(sorted_slots)[:segments]
    got_sums, got_tallies, got_slots = (
        *sent_together(
            (
                partial_value.reshape(groups_x, key_capacity, columns),
                tallies.reshape(groups_x, key_capacity),
            ),
            "gx",
            0,
            0,
            2,
        ),
        lax.all_to_all(
            sent_slots.reshape(groups_x, key_capacity),
            "gx",
            split_axis=0,
            concat_axis=0,
            tiled=True,
        ),
    )
    local_slot = got_slots.reshape(-1) - own_base
    local_slot = jnp.where(got_slots.reshape(-1) >= 0, local_slot, own_slots)
    light_totals, light_tallies, unused_too = one_hot_sums(
        got_sums.reshape(-1, columns), local_slot, own_labels, got_tallies.reshape(-1)
    )
    quarter_totals, quarter_tallies = side_by_side(
        (
            light_totals.reshape(groups_y, key_dev, columns),
            light_tallies.reshape(groups_y, key_dev),
        ),
        "gy",
        0,
        2,
    )
    slot_rows = quarter_tallies.reshape(key_dev)
    inverse = jnp.argsort(key_slot)
    held_keys = lax.dynamic_slice_in_dim(inverse, device * key_dev, key_dev)
    send_order = jnp.argsort(held_keys)
    per_peer = key_dev // groups_x
    moved_totals, moved_tallies = sent_together(
        (
            quarter_totals.reshape(key_dev, columns)[send_order].reshape(
                groups_x, per_peer, columns
            ),
            slot_rows[send_order].reshape(groups_x, per_peer),
        ),
        "gx",
        0,
        0,
        2,
    )
    range_slots = lax.dynamic_slice_in_dim(key_slot, device * key_dev, key_dev)
    arrival = jnp.argsort(range_slots // own_slots, stable=True)
    placed = jnp.argsort(arrival)
    light_sum = moved_totals.reshape(key_dev, columns)[placed]
    light_count = moved_tallies.reshape(key_dev)[placed]
    my_heavy = lax.dynamic_slice_in_dim(heavy_keys, device * heavy_each, heavy_each)
    heavy_local = my_heavy - device * key_dev
    heavy_orders_here = orders[heavy_local]
    shares, share_count = (
        lax.psum_scatter(heavy_part, ("gx", "gy"), scatter_dimension=0, tiled=True),
        lax.psum_scatter(heavy_count, ("gx", "gy"), scatter_dimension=0, tiled=True),
    )
    heavy_value = (
        heavy_orders_here.astype(jnp.float32) * shares * lax.rsqrt(1.0 + share_count)[:, None]
    )
    light_value = orders.astype(jnp.float32) * light_sum * lax.rsqrt(1.0 + light_count)[:, None]
    placing = (heavy_local[:, None] == jnp.arange(key_dev, dtype=jnp.int32)[None, :]).astype(
        jnp.float32
    )
    heavy_full = jnp.sum(placing[:, :, None] * heavy_value[:, None, :], axis=0)
    result = (light_value + heavy_full).astype(jnp.bfloat16)
    return (result, heavy_value.astype(jnp.bfloat16), slot_rows)


def solution(mesh):
    return jax.shard_map(
        body,
        mesh=mesh,
        in_specs=(P(("gx", "gy"), None), P(("gx", "gy")), P(("gx", "gy"), None), P(), P()),
        out_specs=(P(("gx", "gy"), None), P(("gx", "gy"), None), P(("gx", "gy"))),
        check_vma=False,
    )
```

profile of v0, /device:TPU:1, one launch (start us, length us, event | category | flops | bytes accessed | tf_op | source)
XLA Modules:
  0.0 637.5 jit_solution(5043846318612129661)
XLA Ops:
  9.6 22.6 %while.41 = (s32[]{:T(128)}, f32[512,128]{1,0:T(8,128)S(1)}, f32[512]{0:T(512)S(1)}, pred[4,2048]{1,0:T(4,128)(4,1)S(1)}, s32[4,2048]{1,0:T(4,128)S(1)}, /*index...) while((s32[]{:T(128)}, f32[512,128]{1,0:T(8,128)S(1)}, f32[512]{0:T(512)S(1)}, ...), condition=%wide.region_3.4_spmd.clone, body=%wide.region_0.3_spmd.clone.sunk | while | flops 274856448 | bytes 1114736 | solution.py:83
  32.2 45.5 %gather_fusion = s32[8192]{0:T(1024)S(1)} fusion(s32[131072]{0:T(1024)S(1)} %copy-done, s32[8192]{0:T(1024)S(1)} %fusion.35), kind=kCustom, calls=%fused_computation | custom fusion | bytes 98304 | tf_op jit(solution)/shard_map/gather | solution.py:102
  77.8 6.8 %sort.82 = (s32[8192]{0:T(1024)}, s32[8192]{0:T(1024)S(1)}) sort(s32[8192]{0:T(1024)S(1)} %broadcast_select_fusion, s32[8192]{0:T(1024)S(1)} %iota.36), dimensions={0}, to_apply=%region_4.5 | sort | flops 106496 | bytes 131072 | tf_op jit(solution)/shard_map/jit(argsort)/sort | solution.py:107
  84.6 45.5 %gather_fusion.1 = s32[8192]{0:T(1024)S(1)} fusion(s32[8192]{0:T(1024)S(1)} %broadcast_select_fusion, s32[8192]{0:T(1024)S(1)} %get-tuple-element.244), kind=kCustom, calls=%fused_computation.1 | custom fusion | bytes 98304 | tf_op jit(solution)/shard_map/gather | solution.py:108
  131.6 48.9 %gather_fusion.2 = s32[8192]{0:T(1024)S(1)} fusion(s32[65]{0:T(128)S(1)} %convert_reduce_fusion, s32[8192]{0:T(1024)S(1)} %broadcast_clamp_fusion), kind=kCustom, calls=%fused_computation.2 | custom fusion | bytes 98304 | tf_op jit(solution)/shard_map/gather | solution.py:120
  180.6 30.5 %scatter_custom_fusion = s32[4097]{0:T(1024)S(1)} fusion(s32[8192]{0:T(1024)S(1)} %bitcast.93, s32[8192]{0:T(1024)S(1)} %gather_fusion.1, s32[]{:T(128)} %constant.117.clone.1), kind=kCustom, calls=%fused_computation.106 | custom fusion | bytes 16392 | tf_op jit(solution)/shard_map/scatter | solution.py:126
  211.8 13.0 %all-to-all-start = ((s32[64,1,64]{2,1,0:T(1,128)}), s32[64,1,64]{2,1,0:T(1,128)S(1)}, u32[]{:S(2)}, u32[]{:S(2)}) async-start(s32[64,1,64]{2,1,0:T(1,128)} %all_to_all.15), calls=%async_computation | async-start | bytes 65536 | tf_op jit(solution)/shard_map/all_to_all | solution.py:138
  224.8 30.5 %scatter_custom_fusion.1 = s32[8192]{0:T(1024)S(1)} fusion(s32[8192]{0:T(1024)S(1)} %get-tuple-element.243, s32[8192]{0:T(1024)S(1)} %get-tuple-element.235, s32[]{:T(128)} %constant.67.clone.1), kind=kCustom, calls=%fused_computation.103 | custom fusion | bytes 32772 | tf_op jit(solution)/shard_map/scatter | solution.py:122
  255.3 78.7 %while.42 = (s32[]{:T(128)}, f32[4096,128]{1,0:T(8,128)S(1)}, f32[4096]{0:T(1024)S(1)}, s32[4,2048]{1,0:T(4,128)S(1)}, bf16[4,2048,128]{2,1,0:T(8,128)(2,1)}, /*index=5*/s32[]{:T(128)}, s32[]{:T(128)}) while((s32[]{:T(128)}, f32[4096,128]{1,0:T(8,128)S(1)}, f32[4096]{0:T(1024)S(1)}, s32[4,2048]{1,0:T(4,128)S(1)}, ...), condition=%wide.region_11.12_spmd.clone, body=%wide.region_9.11_spmd.clone.sunk | while | flops 2182090752 | bytes 4817500 | solution.py:83
  255.6 11.1 %fusion.69 = f32[4096,128]{1,0:T(8,128)S(1)} fusion(s32[2048]{0:T(1024)S(1)} %bitcast.87, f32[4096,128]{1,0:T(8,128)S(1)} %get-tuple-element.391, pred[]{:T(512)S(6)} %compare.53, bf16[4,2048,128]{2,1,0:T(8,128)(2,1)} %get-tuple-element.401, s32[]{:T(128)} %get-tuple-element.390), kind=kOutput, calls=%fused_computation.30.clone.1 | convolution fusion | flops 2156920832 | bytes 4727297 | tf_op jit(solution)/shard_map/while/body/eval_jaxpr/dot_general | solution.py:70
  266.7 5.3 fusion.70
  272.0 11.1 %fusion.69 = f32[4096,128]{1,0:T(8,128)S(1)} fusion(s32[2048]{0:T(1024)S(1)} %bitcast.87, f32[4096,128]{1,0:T(8,128)S(1)} %get-tuple-element.391, pred[]{:T(512)S(6)} %compare.53, bf16[4,2048,128]{2,1,0:T(8,128)(2,1)} %get-tuple-element.401, s32[]{:T(128)} %get-tuple-element.390), kind=kOutput, calls=%fused_computation.30.clone.1 | convolution fusion | flops 2156920832 | bytes 4727297 | tf_op jit(solution)/shard_map/while/body/eval_jaxpr/dot_general | solution.py:70
  283.1 5.3 fusion.70
  288.4 11.1 %fusion.69 = f32[4096,128]{1,0:T(8,128)S(1)} fusion(s32[2048]{0:T(1024)S(1)} %bitcast.87, f32[4096,128]{1,0:T(8,128)S(1)} %get-tuple-element.391, pred[]{:T(512)S(6)} %compare.53, bf16[4,2048,128]{2,1,0:T(8,128)(2,1)} %get-tuple-element.401, s32[]{:T(128)} %get-tuple-element.390), kind=kOutput, calls=%fused_computation.30.clone.1 | convolution fusion | flops 2156920832 | bytes 4727297 | tf_op jit(solution)/shard_map/while/body/eval_jaxpr/dot_general | solution.py:70
  299.5 5.3 fusion.70
  304.9 11.1 %fusion.69 = f32[4096,128]{1,0:T(8,128)S(1)} fusion(s32[2048]{0:T(1024)S(1)} %bitcast.87, f32[4096,128]{1,0:T(8,128)S(1)} %get-tuple-element.391, pred[]{:T(512)S(6)} %compare.53, bf16[4,2048,128]{2,1,0:T(8,128)(2,1)} %get-tuple-element.401, s32[]{:T(128)} %get-tuple-element.390), kind=kOutput, calls=%fused_computation.30.clone.1 | convolution fusion | flops 2156920832 | bytes 4727297 | tf_op jit(solution)/shard_map/while/body/eval_jaxpr/dot_general | solution.py:70
  315.9 5.3 fusion.70
  337.4 3.9 pad_maximum_fusion
  341.3 10.5 %all-to-all-start.1 = ((f32[64,64,129]{2,1,0:T(8,128)}), f32[64,64,129]{2,1,0:T(8,128)}, u32[]{:S(2)}, u32[]{:S(2)}) async-start(f32[64,64,129]{2,1,0:T(8,128)} %pad_maximum_fusion), calls=%async_computation.1 | async-start | bytes 8388608 | tf_op jit(solution)/shard_map/all_to_all | solution.py:13
  354.3 94.1 %all-to-all-done.1 = f32[64,64,129]{2,1,0:T(8,128)} async-done(((f32[64,64,129]{2,1,0:T(8,128)}), f32[64,64,129]{2,1,0:T(8,128)}, u32[]{:S(2)}, u32[]{:S(2)}) %all-to-all-start.1) | async-done | bytes 2113568 | tf_op jit(solution)/shard_map/all_to_all | solution.py:13
  452.5 32.8 %while.43 = (s32[]{:T(128)}, f32[2048,128]{1,0:T(8,128)S(1)}, f32[2048]{0:T(1024)S(1)}, s32[2,2048]{1,0:T(2,128)S(1)}, f32[2,2048,128]{2,1,0:T(8,128)S(1)}, /*index=5*/f32[2,2048]{1,0:T(2,128)S(1)}, s32[]{:T(128)}, s32[]{:T(128)}) while((s32[]{:T(128)}, f32[2048,128]{1,0:T(8,128)S(1)}, f32[2048]{0:T(1024)S(1)}, ...), condition=%wide.region_15.16_spmd.clone, body=%wide.region_13.15_spmd.clone.sunk | while | flops 6459754496 | bytes 3235948 | solution.py:83
  452.5 13.8 %fusion.72 = f32[2048,128]{1,0:T(8,128)S(1)} fusion(s32[2048]{0:T(1024)S(1)} %bitcast.85, f32[2048,128]{1,0:T(8,128)S(1)} %get-tuple-element.413, f32[2,2048,128]{2,1,0:T(8,128)S(1)} %get-tuple-element.424, s32[]{:T(128)} %get-tuple-element.412, pred[]{:T(512)S(6)} %compare.54), kind=kOutput, calls=%fused_computation.41.clone.1 | convolution fusion | flops 6447169536 | bytes 3153925 | tf_op jit(solution)/shard_map/while/body/eval_jaxpr/dot_general | solution.py:62
  468.8 13.8 %fusion.72 = f32[2048,128]{1,0:T(8,128)S(1)} fusion(s32[2048]{0:T(1024)S(1)} %bitcast.85, f32[2048,128]{1,0:T(8,128)S(1)} %get-tuple-element.413, f32[2,2048,128]{2,1,0:T(8,128)S(1)} %get-tuple-element.424, s32[]{:T(128)} %get-tuple-element.412, pred[]{:T(512)S(6)} %compare.54), kind=kOutput, calls=%fused_computation.41.clone.1 | convolution fusion | flops 6447169536 | bytes 3153925 | tf_op jit(solution)/shard_map/while/body/eval_jaxpr/dot_general | solution.py:62
  489.8 4.2 all-to-all-start.2
  494.8 3.8 sort.85
  498.5 3.8 sort.86
  502.3 76.3 %all-reduce.1 = f32[512]{0:T(512)S(1)} all-reduce(f32[512]{0:T(512)S(1)} %get-tuple-element.129), channel_id=3, replica_groups=mesh['gx'=64,'gy'=4] {'gx','gy'}, use_global_device_ids=true, to_apply=%region_22.23.clone | all-reduce | flops 512 | bytes 4096
  579.4 3.8 sort.84
  585.7 3.5 gather_fusion.4
  590.2 5.4 all-to-all-start.3
  596.3 26.3 %all-reduce.4.cloned.1.call-done = f32[512,128]{1,0:T(8,128)} async-done(((f32[512,128]{1,0:T(8,128)}), f32[512,128]{1,0:T(8,128)}) %all-reduce.4.cloned.1.call-update) | async-done | bytes 262160
  625.4 3.5 gather_fusion.6
  (131 shorter events, 54.7 us)
Async XLA Ops:
  9.6 22.6 %copy-start = (s32[131072]{0:T(1024)S(1)}, s32[131072]{0:T(1024)}, u32[]{:S(2)}) copy-start(s32[131072]{0:T(1024)} %param.15) | copy-start | bytes 1572868
  32.2 45.6 %copy-start.4 = (f32[512,128]{1,0:T(8,128)}, f32[512,128]{1,0:T(8,128)S(1)}, u32[]{:S(2)}) copy-start(f32[512,128]{1,0:T(8,128)S(1)} %get-tuple-element.128) | copy-start | bytes 786436
  211.8 129.5 %all-to-all-start = ((s32[64,1,64]{2,1,0:T(1,128)}), s32[64,1,64]{2,1,0:T(1,128)S(1)}, u32[]{:S(2)}, u32[]{:S(2)}) async-start(s32[64,1,64]{2,1,0:T(1,128)} %all_to_all.15), calls=%async_computation | async-start | bytes 65536 | tf_op jit(solution)/shard_map/all_to_all | solution.py:138
  334.1 1.3 copy-start.2
  341.3 107.1 %all-to-all-start.1 = ((f32[64,64,129]{2,1,0:T(8,128)}), f32[64,64,129]{2,1,0:T(8,128)}, u32[]{:S(2)}, u32[]{:S(2)}) async-start(f32[64,64,129]{2,1,0:T(8,128)} %pad_maximum_fusion), calls=%async_computation.1 | async-start | bytes 8388608 | tf_op jit(solution)/shard_map/all_to_all | solution.py:13
  351.8 226.8 %sort.88.cloned.1.call-start = ((), (), s32[]{:S(2)}) async-start(), calls=%async_computation.5 | async-start | bytes 3145760 | tf_op jit(solution)/shard_map/jit(argsort)/sort | solution.py:161
  352.7 269.9 %all-reduce.4.cloned.1.call-start = ((), (), s32[]{:S(2)}) async-start(), calls=%async_computation.4 | async-start | bytes 524288
  485.3 1.0 copy-start.3
  489.8 93.4 %all-to-all-start.2 = ((f32[4,1,512,129]{2,1,3,0:T(1,128)}), f32[4,1,512,129]{2,1,3,0:T(1,128)S(1)}, u32[]{:S(2)}, u32[]{:S(2)}) async-start(f32[4,1,512,129]{2,1,3,0:T(1,128)} %copy.36), calls=%async_computation.2 | async-start | bytes 2113536 | tf_op jit(solution)/shard_map/all_to_all | solution.py:32
  584.2 11.5 %copy-start.5 = (bf16[512,128]{1,0:T(8,128)(2,1)S(1)}, bf16[512,128]{1,0:T(8,128)(2,1)}, u32[]{:S(2)}) copy-start(bf16[512,128]{1,0:T(8,128)(2,1)} %param.13) | copy-start | bytes 393220
  584.6 40.8 %copy-start.1 = (f32[512]{0:T(512)}, f32[512]{0:T(512)S(1)}, u32[]{:S(2)}) copy-start(f32[512]{0:T(512)S(1)} %slice_reduce_fusion.2) | copy-start | bytes 6148
  590.2 33.8 %all-to-all-start.3 = ((f32[64,8,129]{2,1,0:T(8,128)}), f32[64,8,129]{2,1,0:T(8,128)S(1)}, u32[]{:S(2)}, u32[]{:S(2)}) async-start(f32[64,8,129]{2,1,0:T(8,128)} %pad_maximum_fusion.1), calls=%async_computation.3 | async-start | bytes 1048576 | tf_op jit(solution)/shard_map/all_to_all | solution.py:13
Sparse Core Ops, SparseCore 0:
  355.8 40.6 sort.90.cloned.1.call-done
  (1 shorter events, 0.0 us)
Sparse Core Ops, SparseCore 1:
  358.7 263.9 all-reduce.3
where the time goes:
time: 650 us; the launch traced here: 638 us
  local copies, waits for them, and re-layouts  226 us (35%)
  waiting for transfers between devices  121 us (19%)
  matrix products  82.5 us (13%)
  blocking collectives  76.3 us (12%)
  other arithmetic  68.9 us (11%)
  starting transfers between devices  33.1 us (5%)
  between operations  16.3 us (3%)
  loops' own time  13.8 us (2%)
    all_to_all x2, waiting for transfers between devices, sent_together(): lax.all_to_all(both, axis, split_axis=split_dim, concat_axis=concat_dim,...  94.1 us
    unnamed x1, blocking collectives  76.3 us
    dot_general x8, matrix products, add_block(): lax.dot_general(onehot, block_values, (((0,), (0,)), ((), ())), preferred...  55 us
    gather x1, local copies, waits for them, and re-layouts, body(): before[sorted_owner]  48.9 us
    gather x1, local copies, waits for them, and re-layouts, body(): slot_ids = key_slot[row_keys]  45.5 us
    gather x1, local copies, waits for them, and re-layouts, body(): sorted_slots = sort_keys[ordering]  45.5 us
    reduce_sum x10, other arithmetic, add_block(): jnp.sum(matches.astype(jnp.float32) * block_weights[:, None], axis=0)  31.1 us
    scatter x1, local copies, waits for them, and re-layouts, body(): jnp.full((segments + 1,), -1, jnp.int32).at[segment].set(sorted_slots)  30.5 us
  transfers between devices with their start and end apart: 5, of which 2 were waited for; matrix products, arithmetic and copies ran while one was open for 26% of the time, Pallas kernels for 0%

commit v1 on v0

v1 whole, which is shorter than its diff:
```python
import jax
import jax.numpy as jnp
from jax import lax
from jax.experimental import pallas as pl
from jax.experimental.pallas import tpu as pltpu
from jax.sharding import PartitionSpec as P

F32, BF16, I16, I32 = jnp.float32, jnp.bfloat16, jnp.int16, jnp.int32
LANES = 128
CODE = 32767.0
TINY = 1e-37


def iota(shape, dim, dtype=I32):
    return lax.broadcasted_iota(dtype, shape, dim)


def packed(index):
    return jnp.concatenate([index, index], axis=0).astype(I16)


def hot(count, index):
    n = index.shape[1]
    label = iota((count, n), 0, I16).reshape(count // 16, 16, n)
    return jnp.where(label == index[None], BF16(1), BF16(0)).reshape(count, n)


def mm(a, b):
    return lax.dot_general(a, b, (((1,), (0,)), ((), ())), preferred_element_type=F32)


def mm_nt(a, b):
    return lax.dot_general(a, b, (((1,), (1,)), ((), ())), preferred_element_type=F32)


def flag(mask):
    return jnp.where(mask, 1.0, 0.0).astype(BF16)


def picked(table, index):
    n = index.shape[1]
    hit = iota((LANES, n), 0).reshape(LANES // 8, 8, n) == index[None]
    part = jnp.sum(jnp.where(hit, table.reshape(LANES // 8, 8, n), 0.0), axis=0)
    return jnp.broadcast_to(jnp.sum(part, axis=0, keepdims=True), (8, n))


def exponent(top):
    return jnp.ceil(jnp.log2(jnp.maximum(top, TINY))) + 1.0


def coded(x, shrink):
    y = jnp.sqrt(jnp.sqrt(jnp.abs(x) * shrink)) * CODE + 0.5
    return jnp.where(x < 0, -y, y)


def decoded(code, stretch):
    t = code.astype(F32) * (1.0 / CODE)
    s = t * t
    return s * s * jnp.where(t < 0, -stretch, stretch)


def split2(x):
    high = x.astype(BF16)
    return high, (x - high.astype(F32)).astype(BF16)


def pack_kernel(
    keys_ref, slots_ref, heavy_ref, rows_hbm, out_ref, rows, table, slot_s, place_s, half_s, count_s, meta_s, masked, sem
):
    row_count = rows.shape[0]
    step = 1024
    tiles = step // LANES
    steps = row_count // step
    copy = pltpu.make_async_copy(rows_hbm, rows, sem)
    copy.start()

    slots_t = slots_ref[...].T
    hk = jnp.concatenate([heavy_ref[i : i + 1, :] for i in range(4)], axis=1)
    hk = jnp.broadcast_to(hk, (8, 512))
    weight = (1 + (iota((LANES, 512), 1) & 1)).astype(BF16)
    marks = mm_nt(hot(LANES, packed(hk & 127)) * weight, hot(1024, packed(hk >> 7)))
    table[0:LANES, :] = jnp.where(marks > 0, -marks, (slots_t >> 9).astype(F32)).astype(BF16)
    table[LANES:, :] = jnp.where(marks > 0, 0.0, ((slots_t & 511) - 256).astype(F32)).astype(BF16)
    count_s[...] = jnp.zeros_like(count_s)

    def look_up(t, carry):
        block = keys_ref[pl.ds(t * tiles, tiles), :]
        key = jnp.concatenate([jnp.broadcast_to(block[i : i + 1, :], (8, LANES)) for i in range(tiles)], axis=1)
        found = mm(table[...], hot(1024, packed(key >> 7)))
        high = picked(found[:LANES], key & 127).astype(I32)
        low = picked(found[LANES:], key & 127).astype(I32)
        heavy = high < 0
        slot = jnp.where(heavy, -1 - (2 * (key >> 9) - 1 - high), high * 512 + low + 256)
        slot_s[:, pl.ds(t * step, step)] = slot
        major = jnp.where(heavy, -1, (slot >> 7) & 511)
        minor = ((slot >> 16) & 1) * LANES + (slot & 127)
        count_s[...] += mm_nt(hot(512, packed(major)), hot(256, packed(minor)))
        return carry

    lax.fori_loop(0, steps, look_up, 0)

    present = flag(count_s[...] > 0)
    a, b = iota((256, 512), 0), iota((256, 512), 1)
    b_in = b & 255
    same_half = (a >> 7) == (b_in >> 7)
    both = mm(present, flag(same_half & ((b >= 256) | (a < b_in))))
    a, b = iota((512, 512), 0), iota((512, 512), 1)
    earlier = flag((b < a) & ((a >> 4) == (b >> 4)))
    rank = both[:, :256] + mm(earlier, both[:, 256:].astype(BF16))
    table[0:LANES, 0:512] = rank[:, :LANES].T.astype(BF16)
    table[0:LANES, 512:1024] = rank[:, LANES:].T.astype(BF16)
    meta_s[...] = jnp.zeros_like(meta_s)

    def place(t, carry):
        slot = slot_s[:, pl.ds(t * step, step)]
        light = slot >= 0
        found = mm(table[0:LANES, :], hot(1024, packed(slot >> 7)))
        rank_here = picked(found, slot & 127).astype(I32)
        owner = slot >> 11
        heavy_id = -1 - slot
        at = jnp.where(light, (owner & 31) * 64 + rank_here, 2048 + (heavy_id & 255))
        place_s[:, pl.ds(t * step, step)] = packed(at)
        half = jnp.where(light, owner >> 5, heavy_id >> 8).astype(F32)
        rows_of = jnp.zeros((tiles, LANES), F32)
        for i in range(tiles):
            rows_of = jnp.where(iota((tiles, LANES), 0) == i, half[:, i * LANES : (i + 1) * LANES], rows_of)
        half_s[pl.ds(t * tiles, tiles), :] = rows_of
        owners = hot(64, packed(jnp.where(light, owner, -1)))
        inside = slot & 2047
        high = jnp.broadcast_to((inside >> 6).astype(F32)[0:1], (64, step)).astype(BF16)
        low = jnp.broadcast_to((inside & 63).astype(F32)[0:1], (64, step)).astype(BF16)
        left = jnp.concatenate(
            [owners, owners * high, owners * low, hot(16, packed(jnp.where(light, -1, heavy_id >> 5)))], axis=0
        )
        right = hot(LANES, packed(jnp.where(light, rank_here, 64 + (heavy_id & 31))))
        meta_s[...] += mm_nt(left, right)
        return carry

    lax.fori_loop(0, steps, place, 0)

    copy.wait()
    top = jnp.zeros((16, LANES), BF16)
    for i in range(row_count // 1024):
        piece = jnp.abs(rows[i * 1024 : (i + 1) * 1024, :]).reshape(64, 16, LANES)
        top = jnp.maximum(top, jnp.max(piece, axis=0))
    power = exponent(jnp.max(jnp.max(top.astype(F32), axis=0, keepdims=True), axis=1, keepdims=True))
    shrink_light = jnp.exp2(-8.0 - power)
    shrink_heavy = jnp.exp2(-13.0 - power)
    lane = iota((64, LANES), 1)
    number = meta_s[0:64, :]
    inside = jnp.where(
        number > 0,
        jnp.round(meta_s[64:128, :] / jnp.maximum(number, 1.0)) * 64.0
        + jnp.round(meta_s[128:192, :] / jnp.maximum(number, 1.0)),
        -1.0,
    )
    first = jnp.where(lane < 64, inside, pltpu.roll(number, 64, 1))
    groups = meta_s[192:208, :]
    spread = jnp.concatenate([jnp.broadcast_to(groups[i : i + 1, :], (4, LANES)) for i in range(16)], axis=0)
    owner_row = iota((64, LANES), 0)
    moved = jnp.zeros((64, LANES), F32)
    for c in range(4):
        moved = jnp.where((owner_row & 3) == c, pltpu.roll(spread, 64 - 8 * c, 1), moved)
    moved_high = jnp.floor(moved * (1.0 / 128.0))
    moved_low = moved - 128.0 * moved_high
    second = jnp.where(lane < 8, moved_low, jnp.where(lane < 16, pltpu.roll(moved_high, 8, 1), power))

    half_t = half_s[...].T
    for i in range(row_count // LANES):
        mine = jnp.broadcast_to(half_t[:, i : i + 1], (LANES, LANES)) > 0
        piece = rows[i * LANES : (i + 1) * LANES, :].astype(F32)
        masked[i * LANES : (i + 1) * LANES, 0:LANES] = jnp.where(mine, 0.0, piece).astype(BF16)
        masked[i * LANES : (i + 1) * LANES, LANES:] = jnp.where(mine, piece, 0.0).astype(BF16)

    def block_sums(b):
        total = jnp.zeros((256, 256), F32)
        for c in range(row_count // 2048):
            index = place_s[:, c * 2048 : (c + 1) * 2048] - (b * 256).astype(I16)
            total += mm(hot(256, index), masked[c * 2048 : (c + 1) * 2048, :])
        return total

    def light_block(b, carry):
        total = coded(block_sums(b), shrink_light)
        for h in range(2):
            piece = total[:, h * LANES : (h + 1) * LANES].astype(I32).astype(I16).reshape(4, 64, LANES)
            out_ref[pl.ds(h * 32 + b * 4, 4), 0:64, :] = piece
        return carry

    lax.fori_loop(0, 8, light_block, 0)
    total = coded(block_sums(jnp.int32(8)), shrink_heavy)
    sub = iota((32, 8, LANES), 1)
    for h in range(2):
        own = slice(h * 32, h * 32 + 32)
        sums = total[:, h * LANES : (h + 1) * LANES].reshape(32, 8, LANES)
        extra = jnp.where(sub == 0, first[own][:, None, :], jnp.where(sub == 1, second[own][:, None, :], 0.0))
        out_ref[own, 64:80, :] = jnp.concatenate([sums, extra], axis=1).astype(I32).astype(I16)


def pack(row_keys, key_slot, heavy_keys, measures):
    n = measures.shape[0]
    return pl.pallas_call(
        pack_kernel,
        out_shape=jax.ShapeDtypeStruct((64, 80, LANES), I16),
        in_specs=[pl.BlockSpec(memory_space=pltpu.VMEM)] * 3 + [pl.BlockSpec(memory_space=pl.ANY)],
        scratch_shapes=[
            pltpu.VMEM((n, LANES), BF16),
            pltpu.VMEM((256, 1024), BF16),
            pltpu.VMEM((8, n), I32),
            pltpu.VMEM((16, n), I16),
            pltpu.VMEM((n // LANES, LANES), F32),
            pltpu.VMEM((512, 256), F32),
            pltpu.VMEM((208, LANES), F32),
            pltpu.VMEM((n, 256), BF16),
            pltpu.SemaphoreType.DMA,
        ],
        compiler_params=pltpu.CompilerParams(vmem_limit_bytes=56 * 2**20),
        name="pack",
    )(row_keys.reshape(-1, LANES), key_slot.reshape(-1, LANES), heavy_keys.reshape(-1, LANES), measures)


def label_kernel(me_ref, slots_ref, out_ref):
    slots = slots_ref[...]
    mine = (slots >> 11) == me_ref[0]
    inside = (slots & 2047).astype(F32)
    a, b = iota((LANES, 256), 0), iota((LANES, 256), 1)
    both = mm(flag(mine), flag((b >= LANES) | (a < b)))
    a, b = iota((256, 256), 0), iota((256, 256), 1)
    earlier = flag((b < a) & ((a >> 2) == (b >> 2)))
    lane = iota((256, LANES), 1)
    rows = []
    for c in range(4):
        part = slice(c * 256, (c + 1) * 256)
        rank = both[part, :LANES] + mm(earlier, both[part, LANES:].astype(BF16))
        found = jnp.zeros((256, LANES), F32)
        for j in range(8):
            value = jnp.where(mine[part] & (rank == float(j)), inside[part], 0.0)
            found = jnp.where(lane == j, jnp.sum(value, axis=1, keepdims=True), found)
        rows.append(jnp.sum(found.reshape(64, 4, LANES), axis=1))
    out_ref[...] = jnp.concatenate(rows, axis=0)


def labels_of(index_x, key_slot):
    order = key_slot.reshape(64, 4, 4, LANES).transpose(1, 0, 2, 3).reshape(1024, LANES)
    return pl.pallas_call(
        label_kernel,
        out_shape=jax.ShapeDtypeStruct((256, LANES), F32),
        in_specs=[pl.BlockSpec(memory_space=pltpu.SMEM), pl.BlockSpec(memory_space=pltpu.VMEM)],
        name="labels",
    )(index_x.reshape(1), order)


def owner_kernel(got_ref, label_ref, out_ref, pair_s, index_s, weight_s, sums_s):
    sources = got_ref.shape[0]
    lane = iota((sources, LANES), 1)
    tail = got_ref[:, 64:80, :].astype(F32)
    first = tail[:, 8, :]
    second = tail[:, 9, :]
    stretch = jnp.exp2(tail[:, 9:10, LANES - 1 :] + 8.0)
    heavy = jnp.sum(decoded(tail[:, 0:8, :], stretch * 32.0), axis=0)
    heavy_counts = jnp.sum(second, axis=0, keepdims=True)

    swapped = pltpu.roll(first, 64, 1)
    low_lane = iota((1, LANES), 1) < 64
    for i in range(sources // 2):
        even, odd = slice(2 * i, 2 * i + 1), slice(2 * i + 1, 2 * i + 2)
        at = slice(i * LANES, (i + 1) * LANES)
        index = jnp.where(low_lane, first[even], swapped[odd]).astype(I32)
        index_s[:, at] = packed(jnp.broadcast_to(index, (8, LANES)))
        weight = jnp.where(low_lane, swapped[even], first[odd])
        weight_s[:, at] = jnp.broadcast_to(weight, (16, LANES)).astype(BF16)

    for s in range(0, sources, 8):
        values = decoded(got_ref[s : s + 8, 0:64, :].astype(I32), stretch[s : s + 8]).reshape(512, LANES)
        high, low = split2(values)
        pair_s[s * 64 : (s + 8) * 64, 0:LANES] = high
        pair_s[s * 64 : (s + 8) * 64, LANES:] = low

    index = index_s[...]
    wide = index.astype(I32)[0:8]
    histogram = mm_nt(hot(16, packed(wide >> 7)) * weight_s[...], hot(LANES, packed(wide & 127)))

    top = jnp.max(jnp.abs(heavy), axis=0, keepdims=True)
    for j in range(8):
        column = jnp.broadcast_to(label_ref[:, j : j + 1], (256, LANES)).astype(I32).astype(I16)
        column = column.reshape(16, 16, LANES)
        total = jnp.zeros((256, 256), F32)
        for c in range(0, sources * 64, 1024):
            hots = jnp.concatenate(
                [
                    jnp.where(column == index_s[:, c + i * LANES : c + (i + 1) * LANES][None], BF16(1), BF16(0)).reshape(256, LANES)
                    for i in range(8)
                ],
                axis=1,
            )
            total += mm(hots, pair_s[c : c + 1024, :])
        total = total[:, :LANES] + total[:, LANES:]
        sums_s[j] = total
        top = jnp.maximum(top, jnp.max(jnp.abs(total), axis=0, keepdims=True))

    power = exponent(jnp.max(top, axis=1, keepdims=True))
    shrink = jnp.exp2(-power)
    heavy_code = coded(heavy, shrink)
    for q in range(4):
        for j in range(8):
            out_ref[q, j * 64 : (j + 1) * 64, :] = coded(sums_s[j, q * 64 : (q + 1) * 64, :], shrink).astype(I32).astype(I16)
        extra = jnp.concatenate(
            [
                heavy_code[2 * q : 2 * q + 2],
                histogram[4 * q : 4 * q + 4],
                heavy_counts,
                jnp.broadcast_to(power, (1, LANES)),
                jnp.zeros((8, LANES), F32),
            ],
            axis=0,
        )
        out_ref[q, 512:528, :] = extra.astype(I32).astype(I16)


def owner_sums(got, labels):
    return pl.pallas_call(
        owner_kernel,
        out_shape=jax.ShapeDtypeStruct((4, 528, LANES), I16),
        scratch_shapes=[
            pltpu.VMEM((4096, 256), BF16),
            pltpu.VMEM((16, 4096), I16),
            pltpu.VMEM((16, 4096), BF16),
            pltpu.VMEM((8, 256, LANES), F32),
        ],
        compiler_params=pltpu.CompilerParams(vmem_limit_bytes=56 * 2**20),
        name="owner",
    )(got, labels)


def quarter_kernel(me_ref, got_ref, label_ref, out_ref, rows_ref, own_ref, place_s):
    tail = got_ref[:, 512:528, :].astype(F32)
    stretch = jnp.exp2(tail[:, 7:8, :])
    counts = jnp.sum(tail[:, 2:6, :], axis=0)
    rows_ref[...] = counts
    heavy = jnp.sum(decoded(tail[:, 0:2, :], stretch), axis=0)
    heavy_counts = jnp.sum(tail[:, 6, :], axis=0, keepdims=True)
    own_ref[...] = jnp.concatenate([heavy, heavy_counts, jnp.zeros((5, LANES), F32)], axis=0)

    labels = label_ref[pl.ds(me_ref[0] * 64, 64), :].astype(I32)
    lane = iota((64, LANES), 1)
    found = jnp.zeros((64, LANES), F32)
    top = jnp.zeros((1, LANES), F32)
    for j in range(8):
        total = jnp.zeros((64, LANES), F32)
        for s in range(4):
            total += decoded(got_ref[s, j * 64 : (j + 1) * 64, :].astype(I32), stretch[s])
        place_s[:, j, :] = total
        top = jnp.maximum(top, jnp.max(jnp.abs(total), axis=0, keepdims=True))
        column = jnp.broadcast_to(labels[:, j : j + 1], (64, LANES))
        number = jnp.zeros((64, LANES), F32)
        for i in range(4):
            number += jnp.where(column == lane + i * LANES + 512 * me_ref[0], counts[i : i + 1, :], 0.0)
        found = jnp.where(lane == j, jnp.sum(number, axis=1, keepdims=True), found)

    power = exponent(jnp.max(top, axis=1, keepdims=True))
    high = jnp.floor(found * (1.0 / 128.0))
    low = found - 128.0 * high
    line = jnp.where(lane < 8, low, jnp.where(lane < 16, pltpu.roll(high, 8, 1), jnp.broadcast_to(power, (64, LANES))))
    extra = jnp.where(iota((64, 8, LANES), 1) == 0, line[:, None, :], 0.0)
    codes = coded(place_s[...], jnp.exp2(-power)[:, None, :])
    out_ref[...] = jnp.concatenate([codes, extra], axis=1).astype(I32).astype(I16)


def quarter_sums(index_y, got, labels):
    vmem = pl.BlockSpec(memory_space=pltpu.VMEM)
    return pl.pallas_call(
        quarter_kernel,
        out_shape=(
            jax.ShapeDtypeStruct((64, 16, LANES), I16),
            jax.ShapeDtypeStruct((4, LANES), F32),
            jax.ShapeDtypeStruct((8, LANES), F32),
        ),
        in_specs=[pl.BlockSpec(memory_space=pltpu.SMEM), vmem, vmem],
        scratch_shapes=[pltpu.VMEM((64, 8, LANES), F32)],
        name="quarter",
    )(index_y.reshape(1), got, labels)


def join_kernel(heavy_ref, me_ref, got_ref, own_ref, slots_ref, orders_ref, out_ref, report_ref, joined_s):
    block = got_ref[...].astype(F32)
    sums = decoded(block[:, 0:8, :], jnp.exp2(block[:, 8:9, LANES - 1 :])).reshape(512, LANES)
    lane = iota((64, 8, LANES), 2)
    sub = iota((64, 8, LANES), 1)
    line = jnp.broadcast_to(block[:, 8:9, :], (64, 8, LANES))
    low = jnp.sum(jnp.where(lane == sub, line, 0.0), axis=2, keepdims=True)
    high = jnp.sum(jnp.where(lane == sub + 8, line, 0.0), axis=2, keepdims=True)
    low = jnp.broadcast_to(low, (64, 8, LANES)).reshape(512, LANES).astype(BF16)
    high = jnp.broadcast_to(high * 128.0, (64, 8, LANES)).reshape(512, LANES)
    high_a, high_b = split2(high)
    sum_a, sum_b = split2(sums)
    right = jnp.concatenate([sum_a, sum_b, low, high_a, high_b], axis=1)

    owner = slots_ref[...] >> 11
    wide = jnp.concatenate([jnp.broadcast_to(owner[i : i + 1, :], (8, LANES)) for i in range(4)], axis=1)
    padded = jnp.concatenate([owner, owner], axis=0)
    turned = padded.astype(F32).T.astype(I32)
    earlier = jnp.zeros((8, 512), F32)
    k = iota((16, 8, 512), 2)
    for i in range(4):
        column = jnp.broadcast_to(turned[:, i : i + 1], (LANES, 512)).reshape(16, 8, 512)
        other = iota((LANES, 512), 0).reshape(16, 8, 512) + i * LANES
        earlier += jnp.sum(jnp.where((column == wide[None]) & (other < k), 1.0, 0.0), axis=0)
    place = (wide * 8).astype(F32) + jnp.sum(earlier, axis=0, keepdims=True)
    rows = jnp.concatenate([place[0:1, i * LANES : (i + 1) * LANES] for i in range(4)] * 2, axis=0)
    columns = rows.T
    for i in range(4):
        part = slice(i * LANES, (i + 1) * LANES)
        spot = jnp.broadcast_to(columns[:, i : i + 1], (LANES, 512)).astype(I32)
        moved = mm(flag(spot == iota((LANES, 512), 1)), right)
        total = moved[:, 0:LANES] + moved[:, LANES : 2 * LANES]
        number = moved[:, 2 * LANES : 3 * LANES] + (moved[:, 3 * LANES : 4 * LANES] + moved[:, 4 * LANES :])
        key = iota((LANES, LANES), 0) + i * LANES
        for h in range(2):
            hit = key == heavy_ref[h]
            spot = 2 * me_ref[0] + h
            line = own_ref[2:3, :]
            here = iota((1, LANES), 1)
            count = jnp.sum(
                jnp.where(here == spot, line, 0.0) + jnp.where(here == spot + 8, line * 128.0, 0.0), axis=1, keepdims=True
            )
            total = jnp.where(hit, own_ref[h : h + 1, :], total)
            number = jnp.where(hit, count, number)
        joined = orders_ref[part, :].astype(F32) * total * lax.rsqrt(1.0 + number)
        joined_s[part, :] = joined
        out_ref[part, :] = joined.astype(BF16)
    report_ref[...] = jnp.concatenate(
        [joined_s[pl.ds(heavy_ref[0], 1), :], joined_s[pl.ds(heavy_ref[1], 1), :]], axis=0
    ).astype(BF16)


def join(heavy_here, index_y, got, own, slots_here, orders):
    vmem = pl.BlockSpec(memory_space=pltpu.VMEM)
    smem = pl.BlockSpec(memory_space=pltpu.SMEM)
    return pl.pallas_call(
        join_kernel,
        out_shape=(jax.ShapeDtypeStruct((512, LANES), BF16), jax.ShapeDtypeStruct((2, LANES), BF16)),
        in_specs=[smem, smem, vmem, vmem, vmem, vmem],
        scratch_shapes=[pltpu.VMEM((512, LANES), F32)],
        name="join",
    )(heavy_here, index_y.reshape(1), got, own, slots_here, orders)


def body(measures, row_keys, orders, heavy_keys, key_slot):
    index_x = lax.axis_index("gx")
    index_y = lax.axis_index("gy")
    device = index_x * 4 + index_y
    message = pack(row_keys, key_slot, heavy_keys, measures)
    got = lax.all_to_all(message, "gx", split_axis=0, concat_axis=0, tiled=True)
    labels = labels_of(index_x, key_slot)
    partial = owner_sums(got, labels)
    got = lax.all_to_all(partial, "gy", split_axis=0, concat_axis=0, tiled=True)
    message, slot_rows, own = quarter_sums(index_y, got, labels)
    got = lax.all_to_all(message, "gx", split_axis=0, concat_axis=0, tiled=True)
    heavy_here = lax.dynamic_slice_in_dim(heavy_keys, device * 2, 2) - device * 512
    slots_here = lax.dynamic_slice_in_dim(key_slot, device * 512, 512).reshape(4, LANES)
    result, report = join(heavy_here, index_y, got, own, slots_here, orders)
    return result, report, slot_rows.reshape(512)


def solution(mesh):
    return jax.shard_map(
        body,
        mesh=mesh,
        in_specs=(P(("gx", "gy"), None), P(("gx", "gy")), P(("gx", "gy"), None), P(), P()),
        out_specs=(P(("gx", "gy"), None), P(("gx", "gy"), None), P(("gx", "gy"))),
        check_vma=False,
    )
```

time: 650 us -> 132 us (0.20); the launches traced: 638 us -> 132 us
  local copies, waits for them, and re-layouts: 226 us -> 4.16 us
  matrix products: 82.5 us -> 0 us
  blocking collectives: 76.3 us -> 0 us
  waiting for transfers between devices: 121 us -> 49.5 us
  other arithmetic: 68.9 us -> 1.35 us
  Pallas kernels: 0 us -> 52.4 us
  between operations: 16.3 us -> 0.69 us
  loops' own time: 13.8 us -> 0 us
  starting transfers between devices: 33.1 us -> 23.9 us
    gather x8 -> x0, local copies, waits for them, and re-layouts: 150 us -> none  [the longest x1 48.9 us: body(): before[sorted_owner]]
    dot_general x10 -> x0, matrix products: 82.5 us -> none  [the longest x8 55 us: add_block(): lax.dot_general(onehot, block_values, (((0,), (0,)), ((), ())), preferred...]
    unnamed x1 -> x0, blocking collectives: 76.3 us -> none
    scatter x2 -> x0, local copies, waits for them, and re-layouts: 61 us -> none  [the longest x1 30.5 us: body(): jnp.full((segments + 1,), -1, jnp.int32).at[segment].set(sorted_slots)]
    pallas_call x0 -> x5, Pallas kernels: none -> 52.4 us  [the longest x1 33.6 us: pack(): pl.pallas_call(pack_kernel, out_shape=jax.ShapeDtypeStruct((64, 80, LANES...]
    all_to_all x4 -> x3, waiting for transfers between devices: 94.1 us -> 49.5 us  [the longest x2 39.8 us: body(): got = lax.all_to_all(message, 'gx', split_axis=0, concat_axis=0, tiled=True)]
    reduce_sum x13 -> x0, other arithmetic: 32.8 us -> none  [the longest x10 31.1 us: add_block(): jnp.sum(matches.astype(jnp.float32) * block_weights[:, None], axis=0)]
    unnamed x2 -> x0, waiting for transfers between devices: 26.8 us -> none
  transfers between devices with their start and end apart: 5 -> 3, of which waited for: 2 -> 3; matrix products, arithmetic and copies ran while one was open for 26% -> 2% of each run, Pallas kernels for 0% -> 3%
where the time goes in v1:
time: 132 us
  Pallas kernels  52.4 us (40%)
  waiting for transfers between devices  49.5 us (38%)
  starting transfers between devices  23.9 us (18%)
  local copies, waits for them, and re-layouts  4.16 us (3%)
  other arithmetic  1.35 us (1%)
    all_to_all x2, waiting for transfers between devices, body(): got = lax.all_to_all(message, 'gx', split_axis=0, concat_axis=0, tiled=True)  39.8 us
    pallas_call x1, Pallas kernels, pack(): pl.pallas_call(pack_kernel, out_shape=jax.ShapeDtypeStruct((64, 80, LANES...  33.6 us
    all_to_all x2, starting transfers between devices, body(): got = lax.all_to_all(message, 'gx', split_axis=0, concat_axis=0, tiled=True)  19.7 us
    all_to_all x1, waiting for transfers between devices, body(): got = lax.all_to_all(partial, 'gy', split_axis=0, concat_axis=0, tiled=True)  9.66 us
    pallas_call x1, Pallas kernels, owner_sums(): pl.pallas_call(owner_kernel, out_shape=jax.ShapeDtypeStruct((4, 528, LANE...  8.59 us
    all_to_all x1, starting transfers between devices, body(): got = lax.all_to_all(partial, 'gy', split_axis=0, concat_axis=0, tiled=True)  4.19 us
    pallas_call x1, Pallas kernels, join(): pl.pallas_call(join_kernel, out_shape=(jax.ShapeDtypeStruct((512, LANES),...  3.77 us
    pallas_call x1, Pallas kernels, labels_of(): pl.pallas_call(label_kernel, out_shape=jax.ShapeDtypeStruct((256, LANES),...  3.35 us
  transfers between devices with their start and end apart: 3, of which 3 were waited for; matrix products, arithmetic and copies ran while one was open for 2% of the time, Pallas kernels for 3%

profile of v1, /device:TPU:1, one launch (start us, length us, event | category | flops | bytes accessed | tf_op | source)
XLA Modules:
  0.0 131.9 jit_solution(1174653024514028200)
XLA Ops:
  0.6 33.6 %pack.1 = s16[64,80,128]{2,1,0:T(8,128)(2,1)} custom-call(s32[64,128]{1,0:T(8,128)} %bitcast.15, s32[1024,128]{1,0:T(8,128)} %bitcast.12, s32[4,128]{1,0:T(4,128)} %bitcast.16, bf16[8192,128]{1,0:T(8,128)(2,1)} %rows_hbm.1), custom_call_target="tpu_custom_call" | custom-call | tf_op jit(solution)/shard_map/pack/pallas_call | solution.py:201
  34.2 0.0 copy-start.2
  34.2 13.1 %all-to-all-start = ((s16[64,80,128]{2,1,0:T(8,128)(2,1)}), s16[64,80,128]{2,1,0:T(8,128)(2,1)S(1)}, u32[]{:S(2)}, u32[]{:S(2)}) async-start(s16[64,80,128]{2,1,0:T(8,128)(2,1)} %pack.1), calls=%async_computation | async-start | bytes 2621440 | tf_op jit(solution)/shard_map/all_to_all | solution.py:452
  47.4 0.0 copy-done.2
  47.4 0.9 copy.8
  48.3 3.3 %labels.1.label_ref = f32[256,128]{1,0:T(8,128)} custom-call(s32[1]{0:T(128)} %bitcast.4.me_ref, s32[1024,128]{1,0:T(8,128)} %bitcast.14), custom_call_target="tpu_custom_call" | custom-call | tf_op jit(solution)/shard_map/labels/pallas_call | solution.py:244
  51.6 29.9 %all-to-all-done.got_ref = s16[64,80,128]{2,1,0:T(8,128)(2,1)S(1)} async-done(((s16[64,80,128]{2,1,0:T(8,128)(2,1)}), s16[64,80,128]{2,1,0:T(8,128)(2,1)S(1)}, u32[]{:S(2)}, u32[]{:S(2)}) %all-to-all-start) | async-done | bytes 1310752 | tf_op jit(solution)/shard_map/all_to_all | solution.py:452
  81.5 0.0 copy-start
  81.5 1.1 copy-done
  82.6 8.6 %owner.1 = s16[4,528,128]{2,1,0:T(8,128)(2,1)} custom-call(s16[64,80,128]{2,1,0:T(8,128)(2,1)} %copy-done, f32[256,128]{1,0:T(8,128)} %labels.1.label_ref), custom_call_target="tpu_custom_call" | custom-call | tf_op jit(solution)/shard_map/owner/pallas_call | solution.py:320
  91.2 4.2 %all-to-all-start.1 = ((s16[4,528,128]{2,1,0:T(8,128)(2,1)}), s16[4,528,128]{2,1,0:T(8,128)(2,1)S(1)}, u32[]{:S(2)}, u32[]{:S(2)}) async-start(s16[4,528,128]{2,1,0:T(8,128)(2,1)} %owner.1), calls=%async_computation.1 | async-start | bytes 1081344 | tf_op jit(solution)/shard_map/all_to_all | solution.py:455
  95.4 9.7 %all-to-all-done.1.got_ref = s16[4,528,128]{2,1,0:T(8,128)(2,1)S(1)} async-done(((s16[4,528,128]{2,1,0:T(8,128)(2,1)}), s16[4,528,128]{2,1,0:T(8,128)(2,1)S(1)}, u32[]{:S(2)}, u32[]{:S(2)}) %all-to-all-start.1) | async-done | bytes 540704 | tf_op jit(solution)/shard_map/all_to_all | solution.py:455
  105.0 0.0 copy-start.1
  105.0 0.8 copy-done.1
  105.8 3.1 %quarter.1 = (s16[64,16,128]{2,1,0:T(8,128)(2,1)}, f32[4,128]{1,0:T(4,128)}, f32[8,128]{1,0:T(8,128)}) custom-call(s32[1]{0:T(128)} %bitcast.me_ref, s16[4,528,128]{2,1,0:T(8,128)(2,1)} %copy-done.1, f32[256,128]{1,0:T(8,128)} %labels.1.label_ref), custom_call_target="tpu_custom_call" | custom-call | tf_op jit(solution)/shard_map/quarter/pallas_call | solution.py:370
  108.9 6.6 %all-to-all-start.2 = ((s16[64,16,128]{2,1,0:T(8,128)(2,1)}), s16[64,16,128]{2,1,0:T(8,128)(2,1)S(1)}, u32[]{:S(2)}, u32[]{:S(2)}) async-start(s16[64,16,128]{2,1,0:T(8,128)(2,1)} %get-tuple-element.8), calls=%async_computation.2 | async-start | bytes 524288 | tf_op jit(solution)/shard_map/all_to_all | solution.py:457
  115.5 1.3 %dynamic-slice_subtract_fusion.heavy_ref = s32[2]{0:T(128)} fusion(s32[512]{0:T(512)} %param.8, s32[]{:T(128)S(6)} %select_n.6, s32[]{:T(128)S(6)} %mul.12), kind=kLoop, calls=%fused_computation.1 | loop fusion | flops 2 | bytes 24 | tf_op jit(solution)/shard_map/sub | solution.py:458
  116.9 0.7 dynamic-slice_bitcast_fusion.slots_ref
  117.5 10.0 %all-to-all-done.2.got_ref = s16[64,16,128]{2,1,0:T(8,128)(2,1)S(1)} async-done(((s16[64,16,128]{2,1,0:T(8,128)(2,1)}), s16[64,16,128]{2,1,0:T(8,128)(2,1)S(1)}, u32[]{:S(2)}, u32[]{:S(2)}) %all-to-all-start.2) | async-done | bytes 262176 | tf_op jit(solution)/shard_map/all_to_all | solution.py:457
  127.5 0.0 copy-start.3
  127.5 0.7 copy-done.3
  128.2 3.8 %join.1 = (bf16[512,128]{1,0:T(8,128)(2,1)}, bf16[2,128]{1,0:T(2,128)(2,1)}) custom-call(s32[2]{0:T(128)} %dynamic-slice_subtract_fusion.heavy_ref, s32[1]{0:T(128)} %bitcast.me_ref, s16[64,16,128]{2,1,0:T(8,128)(2,1)} %copy-done.3, f32[8,128]{1,0:T(8,128)} %get-tuple-element.9.own_ref, s32[4,128]{1,0:T(4,128)} %dynamic-slice_bitcast_fusion.slots_ref, ...), custom_call_target="tpu_custom_call" | custom-call | tf_op jit(solution)/shard_map/join/pallas_call | solution.py:438
Async XLA Ops:
  34.2 13.2 %copy-start.2 = (s32[131072]{0:T(1024)S(1)}, s32[131072]{0:T(1024)}, u32[]{:S(2)}) copy-start(s32[131072]{0:T(1024)} %param.9) | copy-start | bytes 1572868
  34.2 47.3 %all-to-all-start = ((s16[64,80,128]{2,1,0:T(8,128)(2,1)}), s16[64,80,128]{2,1,0:T(8,128)(2,1)S(1)}, u32[]{:S(2)}, u32[]{:S(2)}) async-start(s16[64,80,128]{2,1,0:T(8,128)(2,1)} %pack.1), calls=%async_computation | async-start | bytes 2621440 | tf_op jit(solution)/shard_map/all_to_all | solution.py:452
  81.5 1.1 copy-start
  91.2 13.8 %all-to-all-start.1 = ((s16[4,528,128]{2,1,0:T(8,128)(2,1)}), s16[4,528,128]{2,1,0:T(8,128)(2,1)S(1)}, u32[]{:S(2)}, u32[]{:S(2)}) async-start(s16[4,528,128]{2,1,0:T(8,128)(2,1)} %owner.1), calls=%async_computation.1 | async-start | bytes 1081344 | tf_op jit(solution)/shard_map/all_to_all | solution.py:455
  105.0 0.8 copy-start.1
  108.9 18.6 %all-to-all-start.2 = ((s16[64,16,128]{2,1,0:T(8,128)(2,1)}), s16[64,16,128]{2,1,0:T(8,128)(2,1)S(1)}, u32[]{:S(2)}, u32[]{:S(2)}) async-start(s16[64,16,128]{2,1,0:T(8,128)(2,1)} %get-tuple-element.8), calls=%async_computation.2 | async-start | bytes 524288 | tf_op jit(solution)/shard_map/all_to_all | solution.py:457
  127.5 0.7 copy-start.3

commit v2 on v1

--- a/solution.py
+++ b/solution.py
@@ -3,12 +3,19 @@
 from jax import lax
 from jax.experimental import pallas as pl
 from jax.experimental.pallas import tpu as pltpu
+from jax.sharding import Mesh
 from jax.sharding import PartitionSpec as P
 
 F32, BF16, I16, I32 = jnp.float32, jnp.bfloat16, jnp.int16, jnp.int32
 LANES = 128
 CODE = 32767.0
 TINY = 1e-37
+AXES = ("x", "t", "low", "core", "y")
+GROUP = ("x", "low", "core", "y")
+
+
+def near(x):
+    return pltpu.with_memory_space_constraint(x, pltpu.VMEM)
 
 
 def iota(shape, dim, dtype=I32):
@@ -62,6 +69,10 @@
 def split2(x):
     high = x.astype(BF16)
     return high, (x - high.astype(F32)).astype(BF16)
+
+
+def peer_of(owner):
+    return (owner & 48) | ((owner & 3) << 2) | ((owner >> 2) & 3)
 
 
 def pack_kernel(
@@ -117,15 +128,18 @@
         found = mm(table[0:LANES, :], hot(1024, packed(slot >> 7)))
         rank_here = picked(found, slot & 127).astype(I32)
         owner = slot >> 11
+        peer = peer_of(owner)
         heavy_id = -1 - slot
-        at = jnp.where(light, (owner & 31) * 64 + rank_here, 2048 + (heavy_id & 255))
+        heavy_peer = peer_of(heavy_id >> 3) & 60 | (heavy_id >> 1) & 3
+        heavy_id = heavy_peer * 8 + ((heavy_id >> 5) & 3) * 2 + (heavy_id & 1)
+        at = jnp.where(light, (peer & 31) * 64 + rank_here, 2048 + (heavy_id & 255))
         place_s[:, pl.ds(t * step, step)] = packed(at)
-        half = jnp.where(light, owner >> 5, heavy_id >> 8).astype(F32)
+        half = jnp.where(light, peer >> 5, heavy_id >> 8).astype(F32)
         rows_of = jnp.zeros((tiles, LANES), F32)
         for i in range(tiles):
             rows_of = jnp.where(iota((tiles, LANES), 0) == i, half[:, i * LANES : (i + 1) * LANES], rows_of)
         half_s[pl.ds(t * tiles, tiles), :] = rows_of
-        owners = hot(64, packed(jnp.where(light, owner, -1)))
+        owners = hot(64, packed(jnp.where(light, peer, -1)))
         inside = slot & 2047
         high = jnp.broadcast_to((inside >> 6).astype(F32)[0:1], (64, step)).astype(BF16)
         low = jnp.broadcast_to((inside & 63).astype(F32)[0:1], (64, step)).astype(BF16)
@@ -200,7 +214,7 @@
     n = measures.shape[0]
     return pl.pallas_call(
         pack_kernel,
-        out_shape=jax.ShapeDtypeStruct((64, 80, LANES), I16),
+        out_shape=pltpu.VMEM((64, 80, LANES), I16),
         in_specs=[pl.BlockSpec(memory_space=pltpu.VMEM)] * 3 + [pl.BlockSpec(memory_space=pl.ANY)],
         scratch_shapes=[
             pltpu.VMEM((n, LANES), BF16),
@@ -239,19 +253,34 @@
     out_ref[...] = jnp.concatenate(rows, axis=0)
 
 
-def labels_of(index_x, key_slot):
-    order = key_slot.reshape(64, 4, 4, LANES).transpose(1, 0, 2, 3).reshape(1024, LANES)
+def labels_of(owner, key_slot):
+    order = key_slot.reshape(4, 4, 16, 4, LANES).transpose(1, 0, 2, 3, 4).reshape(1024, LANES)
     return pl.pallas_call(
         label_kernel,
-        out_shape=jax.ShapeDtypeStruct((256, LANES), F32),
+        out_shape=pltpu.VMEM((256, LANES), F32),
         in_specs=[pl.BlockSpec(memory_space=pltpu.SMEM), pl.BlockSpec(memory_space=pltpu.VMEM)],
         name="labels",
-    )(index_x.reshape(1), order)
-
-
-def owner_kernel(got_ref, label_ref, out_ref, pair_s, index_s, weight_s, sums_s):
+    )(owner.reshape(1), order)
+
+
+def slot_sums(labels, index_s, pair_s):
+    column = jnp.concatenate([jnp.broadcast_to(labels[:, j : j + 1], (64, LANES)) for j in range(8)], axis=0)
+    column = column.astype(I32).astype(I16).reshape(32, 16, LANES)
+    total = jnp.zeros((512, 256), F32)
+    for c in range(0, 4096, 1024):
+        hots = jnp.concatenate(
+            [
+                jnp.where(column == index_s[:, c + i : c + i + LANES][None], BF16(1), BF16(0)).reshape(512, LANES)
+                for i in range(0, 1024, LANES)
+            ],
+            axis=1,
+        )
+        total += mm(hots, pair_s[c : c + 1024, :])
+    return total[:, :LANES] + total[:, LANES:]
+
+
+def owner_kernel(me_ref, got_ref, label_ref, a_ref, b_ref, c_ref, own_ref, pair_s, index_s, weight_s):
     sources = got_ref.shape[0]
-    lane = iota((sources, LANES), 1)
     tail = got_ref[:, 64:80, :].astype(F32)
     first = tail[:, 8, :]
     second = tail[:, 9, :]
@@ -275,70 +304,58 @@
         pair_s[s * 64 : (s + 8) * 64, 0:LANES] = high
         pair_s[s * 64 : (s + 8) * 64, LANES:] = low
 
-    index = index_s[...]
-    wide = index.astype(I32)[0:8]
+    wide = index_s[...].astype(I32)[0:8]
     histogram = mm_nt(hot(16, packed(wide >> 7)) * weight_s[...], hot(LANES, packed(wide & 127)))
 
-    top = jnp.max(jnp.abs(heavy), axis=0, keepdims=True)
-    for j in range(8):
-        column = jnp.broadcast_to(label_ref[:, j : j + 1], (256, LANES)).astype(I32).astype(I16)
-        column = column.reshape(16, 16, LANES)
-        total = jnp.zeros((256, 256), F32)
-        for c in range(0, sources * 64, 1024):
-            hots = jnp.concatenate(
-                [
-                    jnp.where(column == index_s[:, c + i * LANES : c + (i + 1) * LANES][None], BF16(1), BF16(0)).reshape(256, LANES)
-                    for i in range(8)
-                ],
-                axis=1,
-            )
-            total += mm(hots, pair_s[c : c + 1024, :])
-        total = total[:, :LANES] + total[:, LANES:]
-        sums_s[j] = total
-        top = jnp.maximum(top, jnp.max(jnp.abs(total), axis=0, keepdims=True))
-
-    power = exponent(jnp.max(top, axis=1, keepdims=True))
-    shrink = jnp.exp2(-power)
-    heavy_code = coded(heavy, shrink)
-    for q in range(4):
-        for j in range(8):
-            out_ref[q, j * 64 : (j + 1) * 64, :] = coded(sums_s[j, q * 64 : (q + 1) * 64, :], shrink).astype(I32).astype(I16)
+    for i, out_ref in enumerate((a_ref, b_ref, c_ref, own_ref)):
+        t = (me_ref[0] + 1 + i) & 3
+        total = slot_sums(label_ref[pl.ds(t * 64, 64), :], index_s, pair_s)
+        heavy_here = heavy[0:2]
+        for p in range(1, 4):
+            heavy_here = jnp.where(t == p, heavy[2 * p : 2 * p + 2], heavy_here)
+        top = jnp.maximum(jnp.max(jnp.abs(total), axis=0, keepdims=True), jnp.max(jnp.abs(heavy_here), axis=0, keepdims=True))
+        power = exponent(jnp.max(top, axis=1, keepdims=True))
+        shrink = jnp.exp2(-power)
+        out_ref[0:512, :] = coded(total, shrink).astype(I32).astype(I16)
         extra = jnp.concatenate(
             [
-                heavy_code[2 * q : 2 * q + 2],
-                histogram[4 * q : 4 * q + 4],
+                histogram,
+                coded(heavy_here, shrink),
                 heavy_counts,
                 jnp.broadcast_to(power, (1, LANES)),
-                jnp.zeros((8, LANES), F32),
+                jnp.zeros((12, LANES), F32),
             ],
             axis=0,
         )
-        out_ref[q, 512:528, :] = extra.astype(I32).astype(I16)
-
-
-def owner_sums(got, labels):
+        out_ref[512:544, :] = extra.astype(I32).astype(I16)
+
+
+def owner_sums(index_t, got, labels):
+    vmem = pl.BlockSpec(memory_space=pltpu.VMEM)
     return pl.pallas_call(
         owner_kernel,
-        out_shape=jax.ShapeDtypeStruct((4, 528, LANES), I16),
-        scratch_shapes=[
-            pltpu.VMEM((4096, 256), BF16),
-            pltpu.VMEM((16, 4096), I16),
-            pltpu.VMEM((16, 4096), BF16),
-            pltpu.VMEM((8, 256, LANES), F32),
-        ],
-        compiler_params=pltpu.CompilerParams(vmem_limit_bytes=56 * 2**20),
+        out_shape=(pltpu.VMEM((544, LANES), I16),) * 4,
+        in_specs=[pl.BlockSpec(memory_space=pltpu.SMEM), vmem, vmem],
+        scratch_shapes=[pltpu.VMEM((4096, 256), BF16), pltpu.VMEM((16, 4096), I16), pltpu.VMEM((16, 4096), BF16)],
+        compiler_params=pltpu.CompilerParams(vmem_limit_bytes=32 * 2**20),
         name="owner",
-    )(got, labels)
-
-
-def quarter_kernel(me_ref, got_ref, label_ref, out_ref, rows_ref, own_ref, place_s):
-    tail = got_ref[:, 512:528, :].astype(F32)
-    stretch = jnp.exp2(tail[:, 7:8, :])
-    counts = jnp.sum(tail[:, 2:6, :], axis=0)
-    rows_ref[...] = counts
-    heavy = jnp.sum(decoded(tail[:, 0:2, :], stretch), axis=0)
-    heavy_counts = jnp.sum(tail[:, 6, :], axis=0, keepdims=True)
+    )(index_t.reshape(1), near(got), near(labels))
+
+
+def quarter_kernel(me_ref, a_ref, b_ref, c_ref, d_ref, label_ref, out_ref, own_ref, r0_ref, r1_ref, r2_ref, r3_ref, place_s):
+    parts = (a_ref, b_ref, c_ref, d_ref)
+    tails = [ref[512:544, :].astype(F32) for ref in parts]
+    stretch = [jnp.exp2(tail[19:20, :]) for tail in tails]
+    counts = sum(tail[0:16, :] for tail in tails)
+    heavy = sum(decoded(tail[16:18, :], s) for tail, s in zip(tails, stretch))
+    heavy_counts = sum(tail[18:19, :] for tail in tails)
     own_ref[...] = jnp.concatenate([heavy, heavy_counts, jnp.zeros((5, LANES), F32)], axis=0)
+    for i, rows_ref in enumerate((r0_ref, r1_ref, r2_ref, r3_ref)):
+        q = (me_ref[0] + i) & 3
+        rows = counts[0:4]
+        for p in range(1, 4):
+            rows = jnp.where(q == p, counts[4 * p : 4 * p + 4], rows)
+        rows_ref[...] = rows
 
     labels = label_ref[pl.ds(me_ref[0] * 64, 64), :].astype(I32)
     lane = iota((64, LANES), 1)
@@ -347,13 +364,13 @@
     for j in range(8):
         total = jnp.zeros((64, LANES), F32)
         for s in range(4):
-            total += decoded(got_ref[s, j * 64 : (j + 1) * 64, :].astype(I32), stretch[s])
+            total += decoded(parts[s][j * 64 : (j + 1) * 64, :].astype(I32), stretch[s])
         place_s[:, j, :] = total
         top = jnp.maximum(top, jnp.max(jnp.abs(total), axis=0, keepdims=True))
         column = jnp.broadcast_to(labels[:, j : j + 1], (64, LANES))
         number = jnp.zeros((64, LANES), F32)
-        for i in range(4):
-            number += jnp.where(column == lane + i * LANES + 512 * me_ref[0], counts[i : i + 1, :], 0.0)
+        for i in range(16):
+            number += jnp.where(column == lane + i * LANES, counts[i : i + 1, :], 0.0)
         found = jnp.where(lane == j, jnp.sum(number, axis=1, keepdims=True), found)
 
     power = exponent(jnp.max(top, axis=1, keepdims=True))
@@ -365,19 +382,16 @@
     out_ref[...] = jnp.concatenate([codes, extra], axis=1).astype(I32).astype(I16)
 
 
-def quarter_sums(index_y, got, labels):
+def quarter_sums(index_t, parts, labels):
     vmem = pl.BlockSpec(memory_space=pltpu.VMEM)
     return pl.pallas_call(
         quarter_kernel,
-        out_shape=(
-            jax.ShapeDtypeStruct((64, 16, LANES), I16),
-            jax.ShapeDtypeStruct((4, LANES), F32),
-            jax.ShapeDtypeStruct((8, LANES), F32),
-        ),
-        in_specs=[pl.BlockSpec(memory_space=pltpu.SMEM), vmem, vmem],
+        out_shape=(pltpu.VMEM((64, 16, LANES), I16), pltpu.VMEM((8, LANES), F32))
+        + (jax.ShapeDtypeStruct((4, LANES), F32),) * 4,
+        in_specs=[pl.BlockSpec(memory_space=pltpu.SMEM)] + [vmem] * 5,
         scratch_shapes=[pltpu.VMEM((64, 8, LANES), F32)],
         name="quarter",
-    )(index_y.reshape(1), got, labels)
+    )(index_t.reshape(1), *[near(part) for part in parts], near(labels))
 
 
 def join_kernel(heavy_ref, me_ref, got_ref, own_ref, slots_ref, orders_ref, out_ref, report_ref, joined_s):
@@ -394,7 +408,7 @@
     sum_a, sum_b = split2(sums)
     right = jnp.concatenate([sum_a, sum_b, low, high_a, high_b], axis=1)
 
-    owner = slots_ref[...] >> 11
+    owner = peer_of(slots_ref[...] >> 11)
     wide = jnp.concatenate([jnp.broadcast_to(owner[i : i + 1, :], (8, LANES)) for i in range(4)], axis=1)
     padded = jnp.concatenate([owner, owner], axis=0)
     turned = padded.astype(F32).T.astype(I32)
@@ -441,31 +455,38 @@
         in_specs=[smem, smem, vmem, vmem, vmem, vmem],
         scratch_shapes=[pltpu.VMEM((512, LANES), F32)],
         name="join",
-    )(heavy_here, index_y.reshape(1), got, own, slots_here, orders)
+    )(heavy_here, index_y.reshape(1), near(got), near(own), slots_here, orders)
+
+
+def swap(x):
+    return lax.all_to_all(x, GROUP, split_axis=0, concat_axis=0, tiled=True)
 
 
 def body(measures, row_keys, orders, heavy_keys, key_slot):
-    index_x = lax.axis_index("gx")
-    index_y = lax.axis_index("gy")
-    device = index_x * 4 + index_y
-    message = pack(row_keys, key_slot, heavy_keys, measures)
-    got = lax.all_to_all(message, "gx", split_axis=0, concat_axis=0, tiled=True)
-    labels = labels_of(index_x, key_slot)
-    partial = owner_sums(got, labels)
-    got = lax.all_to_all(partial, "gy", split_axis=0, concat_axis=0, tiled=True)
-    message, slot_rows, own = quarter_sums(index_y, got, labels)
-    got = lax.all_to_all(message, "gx", split_axis=0, concat_axis=0, tiled=True)
+    x, t, low, core, y = (lax.axis_index(name) for name in AXES)
+    device = (((x * 4 + t) * 2 + low) * 2 + core) * 4 + y
+    owner = ((x * 4 + y) * 2 + low) * 2 + core
+    got = swap(pack(row_keys, key_slot, heavy_keys, measures))
+    labels = labels_of(owner, key_slot)
+    *sent, kept = owner_sums(t, got, labels)
+    parts = [lax.ppermute(part, "t", [(s, (s + 1 + i) % 4) for s in range(4)]) for i, part in enumerate(sent)]
+    message, own, *rows = quarter_sums(t, parts + [kept], labels)
+    got = swap(message)
+    slot_rows = jnp.where(y == t, rows[0], 0.0)
+    for i in range(1, 4):
+        slot_rows += lax.ppermute(rows[i], ("t", "y"), [(5 * s, 4 * s + (s + i) % 4) for s in range(4)])
     heavy_here = lax.dynamic_slice_in_dim(heavy_keys, device * 2, 2) - device * 512
     slots_here = lax.dynamic_slice_in_dim(key_slot, device * 512, 512).reshape(4, LANES)
-    result, report = join(heavy_here, index_y, got, own, slots_here, orders)
+    result, report = join(heavy_here, t, got, own, slots_here, orders)
     return result, report, slot_rows.reshape(512)
 
 
 def solution(mesh):
+    split = Mesh(mesh.devices.reshape(4, 4, 2, 2, 4), AXES)
     return jax.shard_map(
         body,
-        mesh=mesh,
-        in_specs=(P(("gx", "gy"), None), P(("gx", "gy")), P(("gx", "gy"), None), P(), P()),
-        out_specs=(P(("gx", "gy"), None), P(("gx", "gy"), None), P(("gx", "gy"))),
+        mesh=split,
+        in_specs=(P(AXES, None), P(AXES), P(AXES, None), P(), P()),
+        out_specs=(P(AXES, None), P(AXES, None), P(AXES)),
         check_vma=False,
     )

time: 132 us -> 113 us (0.86)
  waiting for transfers between devices: 49.5 us -> 26.8 us
  starting transfers between devices: 23.9 us -> 32.5 us
  Pallas kernels: 52.4 us -> 48.7 us
  local copies, waits for them, and re-layouts: 4.16 us -> 1.5 us
    all_to_all x3 -> x2, waiting for transfers between devices: 49.5 us -> 16 us  [swap(): return lax.all_to_all(x, GROUP, split_axis=0, concat_axis=0, tiled=True)]
    ppermute x0 -> x6, starting transfers between devices: none -> 16.7 us  [the longest x3 9.66 us: body(): lax.ppermute(part, 't', [(s, (s + 1 + i) % 4) for s in range(4)])]
    ppermute x0 -> x6, waiting for transfers between devices: none -> 10.8 us  [the longest x3 10.8 us: body(): lax.ppermute(part, 't', [(s, (s + 1 + i) % 4) for s in range(4)])]
    all_to_all x3 -> x2, starting transfers between devices: 23.9 us -> 15.8 us  [swap(): return lax.all_to_all(x, GROUP, split_axis=0, concat_axis=0, tiled=True)]
    pallas_call x4, Pallas kernels: 48.6 us -> 45 us  [the longest x1 33.7 us: pack(): pl.pallas_call(pack_kernel, out_shape=pltpu.VMEM((64, 80, LANES), I16), i...]
    unnamed x8 -> x2, local copies, waits for them, and re-layouts: 2.61 us -> 0.01 us
  transfers between devices with their start and end apart: 3 -> 8, of which waited for: 3 -> 3; matrix products, arithmetic and copies ran while one was open for 2% -> 4% of each run, Pallas kernels for 3% -> 2%
where the time goes in v2:
time: 113 us
  Pallas kernels  48.7 us (43%)
  starting transfers between devices  32.5 us (29%)
  waiting for transfers between devices  26.8 us (24%)
  other arithmetic  2.54 us (2%)
  local copies, waits for them, and re-layouts  1.5 us (1%)
    pallas_call x1, Pallas kernels, pack(): pl.pallas_call(pack_kernel, out_shape=pltpu.VMEM((64, 80, LANES), I16), i...  33.7 us
    all_to_all x2, waiting for transfers between devices, swap(): return lax.all_to_all(x, GROUP, split_axis=0, concat_axis=0, tiled=True)  16 us
    all_to_all x2, starting transfers between devices, swap(): return lax.all_to_all(x, GROUP, split_axis=0, concat_axis=0, tiled=True)  15.8 us
    ppermute x3, waiting for transfers between devices, body(): lax.ppermute(part, 't', [(s, (s + 1 + i) % 4) for s in range(4)])  10.8 us
    ppermute x3, starting transfers between devices, body(): lax.ppermute(part, 't', [(s, (s + 1 + i) % 4) for s in range(4)])  9.66 us
    ppermute x3, starting transfers between devices, body(): lax.ppermute(rows[i], ('t', 'y'), [(5 * s, 4 * s + (s + i) % 4) for s in...  7.03 us
    pallas_call x1, Pallas kernels, owner_sums(): pl.pallas_call(owner_kernel, out_shape=(pltpu.VMEM((544, LANES), I16),) *...  6.27 us
    pallas_call x1, Pallas kernels, join(): pl.pallas_call(join_kernel, out_shape=(jax.ShapeDtypeStruct((512, LANES),...  3.69 us
  transfers between devices with their start and end apart: 8, of which 3 were waited for; matrix products, arithmetic and copies ran while one was open for 4% of the time, Pallas kernels for 2%

profile of v2, /device:TPU:1, one launch (start us, length us, event | category | flops | bytes accessed | tf_op | source)
XLA Modules:
  0.0 112.8 jit_solution(13771011287567185524)
XLA Ops:
  0.6 33.7 %pack.1 = s16[64,80,128]{2,1,0:T(8,128)(2,1)} custom-call(s32[64,128]{1,0:T(8,128)} %bitcast.16, s32[1024,128]{1,0:T(8,128)} %bitcast.13, s32[4,128]{1,0:T(4,128)} %bitcast.17, bf16[8192,128]{1,0:T(8,128)(2,1)} %rows_hbm.1), custom_call_target="tpu_custom_call" | custom-call | tf_op jit(solution)/shard_map/pack/pallas_call | solution.py:215
  34.3 0.0 copy-start
  34.3 10.5 %all-to-all-start = ((s16[64,80,128]{2,1,0:T(8,128)(2,1)}), s16[64,80,128]{2,1,0:T(8,128)(2,1)S(1)}, u32[]{:S(2)}, u32[]{:S(2)}) async-start(s16[64,80,128]{2,1,0:T(8,128)(2,1)} %pack.1), calls=%async_computation | async-start | bytes 2621440 | tf_op jit(solution)/shard_map/all_to_all | solution.py:462
  44.8 0.0 copy-done
  44.8 0.8 copy.8
  45.7 2.7 %labels.1.label_ref = f32[256,128]{1,0:T(8,128)S(1)} custom-call(s32[1]{0:T(128)} %bitcast.4.me_ref, s32[1024,128]{1,0:T(8,128)} %bitcast.15), custom_call_target="tpu_custom_call" | custom-call | tf_op jit(solution)/shard_map/labels/pallas_call | solution.py:258
  48.4 16.0 %all-to-all-done.got_ref = s16[64,80,128]{2,1,0:T(8,128)(2,1)S(1)} async-done(((s16[64,80,128]{2,1,0:T(8,128)(2,1)}), s16[64,80,128]{2,1,0:T(8,128)(2,1)S(1)}, u32[]{:S(2)}, u32[]{:S(2)}) %all-to-all-start) | async-done | bytes 1310752 | tf_op jit(solution)/shard_map/all_to_all | solution.py:462
  64.4 6.3 %owner.1 = (s16[544,128]{1,0:T(8,128)(2,1)S(1)}, s16[544,128]{1,0:T(8,128)(2,1)S(1)}, s16[544,128]{1,0:T(8,128)(2,1)S(1)}, s16[544,128]{1,0:T(8,128)(2,1)S(1)}) custom-call(s32[1]{0:T(128)} %bitcast.me_ref, s16[64,80,128]{2,1,0:T(8,128)(2,1)S(1)} %all-to-all-done.got_ref, f32[256,128]{1,0:T(8,128)S(1)} %labels.1.label_ref), custom_call_target="tpu_custom_call" | custom-call | tf_op jit(solution)/shard_map/owner/pallas_call | solution.py:335
  70.6 3.1 %collective-permute-start = (s16[544,128]{1,0:T(8,128)(2,1)S(1)}, s16[544,128]{1,0:T(8,128)(2,1)S(1)}, u32[]{:S(2)}, u32[]{:S(2)}) collective-permute-start(s16[544,128]{1,0:T(8,128)(2,1)S(1)} %get-tuple-element.15), channel_id=1, source_target_pairs={{0,16},{16,32},{32,48},{48,0},{1,17},{17,33},{33,49},{49,1},{2,18}... | collective-permute-start | bytes 417800 | tf_op jit(solution)/shard_map/ppermute | solution.py:472
  73.7 4.2 %collective-permute-start.1 = (s16[544,128]{1,0:T(8,128)(2,1)S(1)}, s16[544,128]{1,0:T(8,128)(2,1)S(1)}, u32[]{:S(2)}, u32[]{:S(2)}) collective-permute-start(s16[544,128]{1,0:T(8,128)(2,1)S(1)} %get-tuple-element.16), channel_id=1, source_target_pairs={{0,32},{16,48},{32,0},{48,16},{1,33},{17,49},{33,1},{49,17},{2,34}... | collective-permute-start | bytes 417800 | tf_op jit(solution)/shard_map/ppermute | solution.py:472
  77.9 2.4 %collective-permute-start.2 = (s16[544,128]{1,0:T(8,128)(2,1)S(1)}, s16[544,128]{1,0:T(8,128)(2,1)S(1)}, u32[]{:S(2)}, u32[]{:S(2)}) collective-permute-start(s16[544,128]{1,0:T(8,128)(2,1)S(1)} %get-tuple-element.17), channel_id=1, source_target_pairs={{0,48},{16,0},{32,16},{48,32},{1,49},{17,1},{33,17},{49,33},{2,50}... | collective-permute-start | bytes 417800 | tf_op jit(solution)/shard_map/ppermute | solution.py:472
  80.3 0.0 collective-permute-done.a_ref
  80.3 6.9 %collective-permute-done.1.b_ref = s16[544,128]{1,0:T(8,128)(2,1)S(1)} collective-permute-done((s16[544,128]{1,0:T(8,128)(2,1)S(1)}, s16[544,128]{1,0:T(8,128)(2,1)S(1)}, u32[]{:S(2)}, u32[]{:S(2)}) %collective-permute-start.1) | collective-permute-done | bytes 139296 | tf_op jit(solution)/shard_map/ppermute | solution.py:472
  87.2 3.9 %collective-permute-done.2.c_ref = s16[544,128]{1,0:T(8,128)(2,1)S(1)} collective-permute-done((s16[544,128]{1,0:T(8,128)(2,1)S(1)}, s16[544,128]{1,0:T(8,128)(2,1)S(1)}, u32[]{:S(2)}, u32[]{:S(2)}) %collective-permute-start.2) | collective-permute-done | bytes 139296 | tf_op jit(solution)/shard_map/ppermute | solution.py:472
  91.1 2.4 %quarter.1 = (s16[64,16,128]{2,1,0:T(8,128)(2,1)}, f32[8,128]{1,0:T(8,128)S(1)}, f32[4,128]{1,0:T(4,128)}, f32[4,128]{1,0:T(4,128)}, f32[4,128]{1,0:T(4,128)}, /*index=5*/f32[4,128]{1,0:T(4,128)}) custom-call(s32[1]{0:T(128)} %bitcast.me_ref, s16[544,128]{1,0:T(8,128)(2,1)S(1)} %collective-permute-done.a_ref, ...), custom_call_target="tpu_custom_call" | custom-call | tf_op jit(solution)/shard_map/quarter/pallas_call | solution.py:387
  93.5 5.3 %all-to-all-start.1 = ((s16[64,16,128]{2,1,0:T(8,128)(2,1)}), s16[64,16,128]{2,1,0:T(8,128)(2,1)S(1)}, u32[]{:S(2)}, u32[]{:S(2)}) async-start(s16[64,16,128]{2,1,0:T(8,128)(2,1)} %get-tuple-element.19), calls=%async_computation.1 | async-start | bytes 524288 | tf_op jit(solution)/shard_map/all_to_all | solution.py:462
  98.8 0.7 dynamic-slice_bitcast_fusion.slots_ref
  99.5 4.5 %collective-permute-start.5 = (f32[4,128]{1,0:T(4,128)}, f32[4,128]{1,0:T(4,128)S(1)}, u32[]{:S(2)}, u32[]{:S(2)}) collective-permute-start(f32[4,128]{1,0:T(4,128)} %get-tuple-element.26), channel_id=1, source_target_pairs={{0,3},{17,16},{34,33},{51,50},{4,7},{21,20},{38,37},{55,54},{8,11}... | collective-permute-start | bytes 6152 | tf_op jit(solution)/shard_map/ppermute | solution.py:477
  104.0 1.3 %collective-permute-start.4 = (f32[4,128]{1,0:T(4,128)}, f32[4,128]{1,0:T(4,128)S(1)}, u32[]{:S(2)}, u32[]{:S(2)}) collective-permute-start(f32[4,128]{1,0:T(4,128)} %get-tuple-element.25), channel_id=1, source_target_pairs={{0,2},{17,19},{34,32},{51,49},{4,6},{21,23},{38,36},{55,53},{8,10}... | collective-permute-start | bytes 6152 | tf_op jit(solution)/shard_map/ppermute | solution.py:477
  105.2 1.3 %collective-permute-start.3 = (f32[4,128]{1,0:T(4,128)}, f32[4,128]{1,0:T(4,128)S(1)}, u32[]{:S(2)}, u32[]{:S(2)}) collective-permute-start(f32[4,128]{1,0:T(4,128)} %get-tuple-element.24), channel_id=1, source_target_pairs={{0,1},{17,18},{34,35},{51,48},{4,5},{21,22},{38,39},{55,52},{8,9},... | collective-permute-start | bytes 6152 | tf_op jit(solution)/shard_map/ppermute | solution.py:477
  106.5 1.3 %dynamic-slice_subtract_fusion.heavy_ref = s32[2]{0:T(128)} fusion(s32[512]{0:T(512)} %param.8, s32[]{:T(128)S(6)} %select_n.14, s32[]{:T(128)S(6)} %mul.31), kind=kLoop, calls=%fused_computation.2 | loop fusion | flops 2 | bytes 24 | tf_op jit(solution)/shard_map/sub | solution.py:478
  107.8 0.0 collective-permute-done.5
  107.8 0.0 collective-permute-done.4
  107.8 0.0 collective-permute-done.3
  107.8 1.3 %add_bitcast_fusion = f32[512]{0:T(512)} fusion(f32[4,128]{1,0:T(4,128)S(1)} %collective-permute-done.5, f32[4,128]{1,0:T(4,128)S(1)} %collective-permute-done.4, f32[4,128]{1,0:T(4,128)S(1)} %collective-permute-done.3, f32[4,128]{1,0:T(4,128)} %get-tuple-element.23, pred[]{:T(512)S(6)} %eq.3), kind=kLoop, calls=%fused_computation | loop fusion | flops 2048 | bytes 10241 | tf_op jit(solution)/shard_map/reshape | solution.py:481
  109.1 0.0 all-to-all-done.1.got_ref
  109.1 3.7 %join.1 = (bf16[512,128]{1,0:T(8,128)(2,1)}, bf16[2,128]{1,0:T(2,128)(2,1)}) custom-call(s32[2]{0:T(128)} %dynamic-slice_subtract_fusion.heavy_ref, s32[1]{0:T(128)} %bitcast.me_ref, s16[64,16,128]{2,1,0:T(8,128)(2,1)S(1)} %all-to-all-done.1.got_ref, f32[8,128]{1,0:T(8,128)S(1)} %get-tuple-element.20.own_ref, s32[4,128]{1,0:T(4,128)} %dynamic-slice_bitcast_fusion.slots_ref, ...), custom_call_target="tpu_custom_call" | custom-call | tf_op jit(solution)/shard_map/join/pallas_call | solution.py:452
Async XLA Ops:
  34.3 10.5 %copy-start = (s32[131072]{0:T(1024)S(1)}, s32[131072]{0:T(1024)}, u32[]{:S(2)}) copy-start(s32[131072]{0:T(1024)} %param.9) | copy-start | bytes 1572868
  34.3 30.1 %all-to-all-start = ((s16[64,80,128]{2,1,0:T(8,128)(2,1)}), s16[64,80,128]{2,1,0:T(8,128)(2,1)S(1)}, u32[]{:S(2)}, u32[]{:S(2)}) async-start(s16[64,80,128]{2,1,0:T(8,128)(2,1)} %pack.1), calls=%async_computation | async-start | bytes 2621440 | tf_op jit(solution)/shard_map/all_to_all | solution.py:462
  70.6 9.7 %collective-permute-start = (s16[544,128]{1,0:T(8,128)(2,1)S(1)}, s16[544,128]{1,0:T(8,128)(2,1)S(1)}, u32[]{:S(2)}, u32[]{:S(2)}) collective-permute-start(s16[544,128]{1,0:T(8,128)(2,1)S(1)} %get-tuple-element.15), channel_id=1, source_target_pairs={{0,16},{16,32},{32,48},{48,0},{1,17},{17,33},{33,49},{49,1},{2,18}... | collective-permute-start | bytes 417800 | tf_op jit(solution)/shard_map/ppermute | solution.py:472
  73.7 13.5 %collective-permute-start.1 = (s16[544,128]{1,0:T(8,128)(2,1)S(1)}, s16[544,128]{1,0:T(8,128)(2,1)S(1)}, u32[]{:S(2)}, u32[]{:S(2)}) collective-permute-start(s16[544,128]{1,0:T(8,128)(2,1)S(1)} %get-tuple-element.16), channel_id=1, source_target_pairs={{0,32},{16,48},{32,0},{48,16},{1,33},{17,49},{33,1},{49,17},{2,34}... | collective-permute-start | bytes 417800 | tf_op jit(solution)/shard_map/ppermute | solution.py:472
  77.9 13.2 %collective-permute-start.2 = (s16[544,128]{1,0:T(8,128)(2,1)S(1)}, s16[544,128]{1,0:T(8,128)(2,1)S(1)}, u32[]{:S(2)}, u32[]{:S(2)}) collective-permute-start(s16[544,128]{1,0:T(8,128)(2,1)S(1)} %get-tuple-element.17), channel_id=1, source_target_pairs={{0,48},{16,0},{32,16},{48,32},{1,49},{17,1},{33,17},{49,33},{2,50}... | collective-permute-start | bytes 417800 | tf_op jit(solution)/shard_map/ppermute | solution.py:472
  93.5 15.6 %all-to-all-start.1 = ((s16[64,16,128]{2,1,0:T(8,128)(2,1)}), s16[64,16,128]{2,1,0:T(8,128)(2,1)S(1)}, u32[]{:S(2)}, u32[]{:S(2)}) async-start(s16[64,16,128]{2,1,0:T(8,128)(2,1)} %get-tuple-element.19), calls=%async_computation.1 | async-start | bytes 524288 | tf_op jit(solution)/shard_map/all_to_all | solution.py:462
  99.5 8.3 %collective-permute-start.5 = (f32[4,128]{1,0:T(4,128)}, f32[4,128]{1,0:T(4,128)S(1)}, u32[]{:S(2)}, u32[]{:S(2)}) collective-permute-start(f32[4,128]{1,0:T(4,128)} %get-tuple-element.26), channel_id=1, source_target_pairs={{0,3},{17,16},{34,33},{51,50},{4,7},{21,20},{38,37},{55,54},{8,11}... | collective-permute-start | bytes 6152 | tf_op jit(solution)/shard_map/ppermute | solution.py:477
  104.0 3.9 %collective-permute-start.4 = (f32[4,128]{1,0:T(4,128)}, f32[4,128]{1,0:T(4,128)S(1)}, u32[]{:S(2)}, u32[]{:S(2)}) collective-permute-start(f32[4,128]{1,0:T(4,128)} %get-tuple-element.25), channel_id=1, source_target_pairs={{0,2},{17,19},{34,32},{51,49},{4,6},{21,23},{38,36},{55,53},{8,10}... | collective-permute-start | bytes 6152 | tf_op jit(solution)/shard_map/ppermute | solution.py:477
  105.2 2.6 %collective-permute-start.3 = (f32[4,128]{1,0:T(4,128)}, f32[4,128]{1,0:T(4,128)S(1)}, u32[]{:S(2)}, u32[]{:S(2)}) collective-permute-start(f32[4,128]{1,0:T(4,128)} %get-tuple-element.24), channel_id=1, source_target_pairs={{0,1},{17,18},{34,35},{51,48},{4,5},{21,22},{38,39},{55,52},{8,9},... | collective-permute-start | bytes 6152 | tf_op jit(solution)/shard_map/ppermute | solution.py:477

commit v3 on v2

--- a/solution.py
+++ b/solution.py
@@ -108,7 +108,7 @@
         count_s[...] += mm_nt(hot(512, packed(major)), hot(256, packed(minor)))
         return carry
 
-    lax.fori_loop(0, steps, look_up, 0)
+    lax.fori_loop(0, steps, look_up, 0, unroll=8)
 
     present = flag(count_s[...] > 0)
     a, b = iota((256, 512), 0), iota((256, 512), 1)
@@ -150,7 +150,7 @@
         meta_s[...] += mm_nt(left, right)
         return carry
 
-    lax.fori_loop(0, steps, place, 0)
+    lax.fori_loop(0, steps, place, 0, unroll=8)
 
     copy.wait()
     top = jnp.zeros((16, LANES), BF16)
@@ -181,33 +181,33 @@
 
     half_t = half_s[...].T
     for i in range(row_count // LANES):
-        mine = jnp.broadcast_to(half_t[:, i : i + 1], (LANES, LANES)) > 0
-        piece = rows[i * LANES : (i + 1) * LANES, :].astype(F32)
-        masked[i * LANES : (i + 1) * LANES, 0:LANES] = jnp.where(mine, 0.0, piece).astype(BF16)
-        masked[i * LANES : (i + 1) * LANES, LANES:] = jnp.where(mine, piece, 0.0).astype(BF16)
-
-    def block_sums(b):
-        total = jnp.zeros((256, 256), F32)
-        for c in range(row_count // 2048):
-            index = place_s[:, c * 2048 : (c + 1) * 2048] - (b * 256).astype(I16)
-            total += mm(hot(256, index), masked[c * 2048 : (c + 1) * 2048, :])
+        mine = jnp.broadcast_to(half_t[:, i : i + 1], (LANES, LANES)).astype(BF16)
+        piece = rows[i * LANES : (i + 1) * LANES, :]
+        second_half = piece * mine
+        masked[i * LANES : (i + 1) * LANES, 0:LANES] = piece - second_half
+        masked[i * LANES : (i + 1) * LANES, LANES:] = second_half
+
+    def block_sums(b, count):
+        total = jnp.zeros((count, 256), F32)
+        for c in range(row_count // 1024):
+            index = place_s[:, c * 1024 : (c + 1) * 1024] - (b * count).astype(I16)
+            total += mm(hot(count, index), masked[c * 1024 : (c + 1) * 1024, :])
         return total
 
     def light_block(b, carry):
-        total = coded(block_sums(b), shrink_light)
+        total = coded(block_sums(b, 512), shrink_light)
         for h in range(2):
-            piece = total[:, h * LANES : (h + 1) * LANES].astype(I32).astype(I16).reshape(4, 64, LANES)
-            out_ref[pl.ds(h * 32 + b * 4, 4), 0:64, :] = piece
+            piece = total[:, h * LANES : (h + 1) * LANES].astype(I32).astype(I16).reshape(8, 64, LANES)
+            out_ref[pl.ds(h * 32 + b * 8, 8), 0:64, :] = piece
         return carry
 
-    lax.fori_loop(0, 8, light_block, 0)
-    total = coded(block_sums(jnp.int32(8)), shrink_heavy)
-    sub = iota((32, 8, LANES), 1)
-    for h in range(2):
-        own = slice(h * 32, h * 32 + 32)
-        sums = total[:, h * LANES : (h + 1) * LANES].reshape(32, 8, LANES)
-        extra = jnp.where(sub == 0, first[own][:, None, :], jnp.where(sub == 1, second[own][:, None, :], 0.0))
-        out_ref[own, 64:80, :] = jnp.concatenate([sums, extra], axis=1).astype(I32).astype(I16)
+    lax.fori_loop(0, 4, light_block, 0, unroll=2)
+    total = coded(block_sums(jnp.int32(8), 256), shrink_heavy)
+    turned = jnp.concatenate([total[:, :LANES].T, total[:, LANES:].T], axis=1)
+    sums = jnp.concatenate([turned[:, k * LANES : (k + 1) * LANES].reshape(64, 2, LANES) for k in range(4)], axis=1)
+    sub = iota((64, 8, LANES), 1)
+    extra = jnp.where(sub == 0, first[:, None, :], jnp.where(sub == 1, second[:, None, :], 0.0))
+    out_ref[:, 64:80, :] = jnp.concatenate([sums, extra], axis=1).astype(I32).astype(I16)
 
 
 def pack(row_keys, key_slot, heavy_keys, measures):
@@ -279,7 +279,7 @@
     return total[:, :LANES] + total[:, LANES:]
 
 
-def owner_kernel(me_ref, got_ref, label_ref, a_ref, b_ref, c_ref, own_ref, pair_s, index_s, weight_s):
+def owner_kernel(me_ref, got_ref, label_ref, out_ref, r0_ref, r1_ref, r2_ref, r3_ref, pair_s, index_s, weight_s):
     sources = got_ref.shape[0]
     tail = got_ref[:, 64:80, :].astype(F32)
     first = tail[:, 8, :]
@@ -307,34 +307,66 @@
     wide = index_s[...].astype(I32)[0:8]
     histogram = mm_nt(hot(16, packed(wide >> 7)) * weight_s[...], hot(LANES, packed(wide & 127)))
 
-    for i, out_ref in enumerate((a_ref, b_ref, c_ref, own_ref)):
-        t = (me_ref[0] + 1 + i) & 3
-        total = slot_sums(label_ref[pl.ds(t * 64, 64), :], index_s, pair_s)
-        heavy_here = heavy[0:2]
+    for i, rows_ref in enumerate((r0_ref, r1_ref, r2_ref, r3_ref)):
+        q = (me_ref[0] + i) & 3
+        rows = histogram[0:4]
         for p in range(1, 4):
-            heavy_here = jnp.where(t == p, heavy[2 * p : 2 * p + 2], heavy_here)
-        top = jnp.maximum(jnp.max(jnp.abs(total), axis=0, keepdims=True), jnp.max(jnp.abs(heavy_here), axis=0, keepdims=True))
+            rows = jnp.where(q == p, histogram[4 * p : 4 * p + 4], rows)
+        rows_ref[...] = rows
+
+    heavy_top = jnp.max(jnp.max(jnp.abs(heavy), axis=0, keepdims=True), axis=1, keepdims=True)
+    heavy_power = exponent(heavy_top)
+    heavy_code = coded(heavy, jnp.exp2(-heavy_power))
+    member = iota((64, LANES), 0)
+    heavy_lines = []
+    for c in range(2):
+        line = jnp.broadcast_to(heavy_code[c : c + 1], (64, LANES))
+        for k in range(1, 4):
+            line = jnp.where((member >> 4) == k, heavy_code[2 * k + c : 2 * k + c + 1], line)
+        heavy_lines.append(line)
+    one_lane = iota((1, LANES), 1)
+
+    lane = iota((64, LANES), 1)
+    quarter = iota((64, LANES), 0) & 3
+    lines = []
+    for i in range(4):
+        line = jnp.broadcast_to(histogram[i : i + 1], (64, LANES))
+        for q in range(1, 4):
+            line = jnp.where(quarter == q, histogram[4 * q + i : 4 * q + i + 1], line)
+        lines.append(line)
+    for t in range(4):
+        labels = label_ref[t * 64 : (t + 1) * 64, :]
+        total = slot_sums(labels, index_s, pair_s)
+        top = jnp.max(jnp.abs(total), axis=0, keepdims=True)
         power = exponent(jnp.max(top, axis=1, keepdims=True))
-        shrink = jnp.exp2(-power)
-        out_ref[0:512, :] = coded(total, shrink).astype(I32).astype(I16)
-        extra = jnp.concatenate(
-            [
-                histogram,
-                coded(heavy_here, shrink),
-                heavy_counts,
-                jnp.broadcast_to(power, (1, LANES)),
-                jnp.zeros((12, LANES), F32),
-            ],
-            axis=0,
-        )
-        out_ref[512:544, :] = extra.astype(I32).astype(I16)
+        code = coded(total, jnp.exp2(-power)).astype(I32)
+        for j in range(4):
+            word = (code[j * 64 : (j + 1) * 64] << 16) | (code[(j + 4) * 64 : (j + 5) * 64] & 65535)
+            out_ref[pl.ds(t * 320 + j, 64, stride=5), :] = word
+        inside = labels.astype(I32) & 511
+        found = jnp.broadcast_to(power, (64, LANES))
+        for j in range(8):
+            column = jnp.broadcast_to(inside[:, j : j + 1], (64, LANES))
+            number = jnp.zeros((64, LANES), F32)
+            for i in range(4):
+                number += jnp.where(column == lane + i * LANES, lines[i], 0.0)
+            found = jnp.where(lane == j, jnp.sum(number, axis=1, keepdims=True), found)
+        found = jnp.where(lane == 126, heavy_power, found).astype(I32)
+        for h in range(2):
+            spot = t * 2 + h
+            hit = lane == (member & 15) * 8 + spot
+            code = [jnp.sum(jnp.where(hit, line, 0.0), axis=1, keepdims=True).astype(I32) for line in heavy_lines]
+            count = jnp.where(one_lane == spot, heavy_counts, 0.0) + jnp.where(one_lane == spot + 8, heavy_counts * 128.0, 0.0)
+            count = jnp.sum(count, axis=1, keepdims=True).astype(I32)
+            found = jnp.where(lane == 8 + h, (code[0] << 16) | (code[1] & 65535), jnp.where(lane == 10 + h, count, found))
+        out_ref[pl.ds(t * 320 + 4, 64, stride=5), :] = found
 
 
 def owner_sums(index_t, got, labels):
     vmem = pl.BlockSpec(memory_space=pltpu.VMEM)
     return pl.pallas_call(
         owner_kernel,
-        out_shape=(pltpu.VMEM((544, LANES), I16),) * 4,
+        out_shape=(pltpu.VMEM((1280, LANES), I32),) + (jax.ShapeDtypeStruct((4, LANES), F32),) * 4,
         in_specs=[pl.BlockSpec(memory_space=pltpu.SMEM), vmem, vmem],
         scratch_shapes=[pltpu.VMEM((4096, 256), BF16), pltpu.VMEM((16, 4096), I16), pltpu.VMEM((16, 4096), BF16)],
         compiler_params=pltpu.CompilerParams(vmem_limit_bytes=32 * 2**20),
@@ -342,72 +374,7 @@
     )(index_t.reshape(1), near(got), near(labels))
 
 
-def quarter_kernel(me_ref, a_ref, b_ref, c_ref, d_ref, label_ref, out_ref, own_ref, r0_ref, r1_ref, r2_ref, r3_ref, place_s):
-    parts = (a_ref, b_ref, c_ref, d_ref)
-    tails = [ref[512:544, :].astype(F32) for ref in parts]
-    stretch = [jnp.exp2(tail[19:20, :]) for tail in tails]
-    counts = sum(tail[0:16, :] for tail in tails)
-    heavy = sum(decoded(tail[16:18, :], s) for tail, s in zip(tails, stretch))
-    heavy_counts = sum(tail[18:19, :] for tail in tails)
-    own_ref[...] = jnp.concatenate([heavy, heavy_counts, jnp.zeros((5, LANES), F32)], axis=0)
-    for i, rows_ref in enumerate((r0_ref, r1_ref, r2_ref, r3_ref)):
-        q = (me_ref[0] + i) & 3
-        rows = counts[0:4]
-        for p in range(1, 4):
-            rows = jnp.where(q == p, counts[4 * p : 4 * p + 4], rows)
-        rows_ref[...] = rows
-
-    labels = label_ref[pl.ds(me_ref[0] * 64, 64), :].astype(I32)
-    lane = iota((64, LANES), 1)
-    found = jnp.zeros((64, LANES), F32)
-    top = jnp.zeros((1, LANES), F32)
-    for j in range(8):
-        total = jnp.zeros((64, LANES), F32)
-        for s in range(4):
-            total += decoded(parts[s][j * 64 : (j + 1) * 64, :].astype(I32), stretch[s])
-        place_s[:, j, :] = total
-        top = jnp.maximum(top, jnp.max(jnp.abs(total), axis=0, keepdims=True))
-        column = jnp.broadcast_to(labels[:, j : j + 1], (64, LANES))
-        number = jnp.zeros((64, LANES), F32)
-        for i in range(16):
-            number += jnp.where(column == lane + i * LANES, counts[i : i + 1, :], 0.0)
-        found = jnp.where(lane == j, jnp.sum(number, axis=1, keepdims=True), found)
-
-    power = exponent(jnp.max(top, axis=1, keepdims=True))
-    high = jnp.floor(found * (1.0 / 128.0))
-    low = found - 128.0 * high
-    line = jnp.where(lane < 8, low, jnp.where(lane < 16, pltpu.roll(high, 8, 1), jnp.broadcast_to(power, (64, LANES))))
-    extra = jnp.where(iota((64, 8, LANES), 1) == 0, line[:, None, :], 0.0)
-    codes = coded(place_s[...], jnp.exp2(-power)[:, None, :])
-    out_ref[...] = jnp.concatenate([codes, extra], axis=1).astype(I32).astype(I16)
-
-
-def quarter_sums(index_t, parts, labels):
-    vmem = pl.BlockSpec(memory_space=pltpu.VMEM)
-    return pl.pallas_call(
-        quarter_kernel,
-        out_shape=(pltpu.VMEM((64, 16, LANES), I16), pltpu.VMEM((8, LANES), F32))
-        + (jax.ShapeDtypeStruct((4, LANES), F32),) * 4,
-        in_specs=[pl.BlockSpec(memory_space=pltpu.SMEM)] + [vmem] * 5,
-        scratch_shapes=[pltpu.VMEM((64, 8, LANES), F32)],
-        name="quarter",
-    )(index_t.reshape(1), *[near(part) for part in parts], near(labels))
-
-
-def join_kernel(heavy_ref, me_ref, got_ref, own_ref, slots_ref, orders_ref, out_ref, report_ref, joined_s):
-    block = got_ref[...].astype(F32)
-    sums = decoded(block[:, 0:8, :], jnp.exp2(block[:, 8:9, LANES - 1 :])).reshape(512, LANES)
-    lane = iota((64, 8, LANES), 2)
-    sub = iota((64, 8, LANES), 1)
-    line = jnp.broadcast_to(block[:, 8:9, :], (64, 8, LANES))
-    low = jnp.sum(jnp.where(lane == sub, line, 0.0), axis=2, keepdims=True)
-    high = jnp.sum(jnp.where(lane == sub + 8, line, 0.0), axis=2, keepdims=True)
-    low = jnp.broadcast_to(low, (64, 8, LANES)).reshape(512, LANES).astype(BF16)
-    high = jnp.broadcast_to(high * 128.0, (64, 8, LANES)).reshape(512, LANES)
-    high_a, high_b = split2(high)
-    sum_a, sum_b = split2(sums)
-    right = jnp.concatenate([sum_a, sum_b, low, high_a, high_b], axis=1)
-
+def place_kernel(slots_ref, out_ref):
     owner = peer_of(slots_ref[...] >> 11)
     wide = jnp.concatenate([jnp.broadcast_to(owner[i : i + 1, :], (8, LANES)) for i in range(4)], axis=1)
     padded = jnp.concatenate([owner, owner], axis=0)
@@ -418,26 +385,59 @@
         column = jnp.broadcast_to(turned[:, i : i + 1], (LANES, 512)).reshape(16, 8, 512)
         other = iota((LANES, 512), 0).reshape(16, 8, 512) + i * LANES
         earlier += jnp.sum(jnp.where((column == wide[None]) & (other < k), 1.0, 0.0), axis=0)
-    place = (wide * 8).astype(F32) + jnp.sum(earlier, axis=0, keepdims=True)
+    place = wide.astype(F32) + 64.0 * jnp.sum(earlier, axis=0, keepdims=True)
     rows = jnp.concatenate([place[0:1, i * LANES : (i + 1) * LANES] for i in range(4)] * 2, axis=0)
     columns = rows.T
     for i in range(4):
+        spot = jnp.broadcast_to(columns[:, i : i + 1], (LANES, 512)).astype(I32)
+        out_ref[i * LANES : (i + 1) * LANES, :] = flag(spot == iota((LANES, 512), 1))
+
+
+def places(slots_here):
+    return pl.pallas_call(place_kernel, out_shape=pltpu.VMEM((512, 512), BF16), name="places")(slots_here)
+
+
+def join_kernel(heavy_ref, me_ref, got_ref, place_ref, orders_ref, out_ref, report_ref, joined_s):
+    lines = [got_ref[pl.ds(t * 320 + 4, 64, stride=5), :] for t in range(4)]
+    stretch = [jnp.exp2(line[:, LANES - 1 :].astype(F32)) for line in lines]
+    found = (lines[0] + lines[1] + lines[2] + lines[3]).astype(F32)
+    lane, member = iota((64, LANES), 1), iota((64, LANES), 0)
+    heavy_sums, heavy_counts = [], []
+    for h in range(2):
+        row = jnp.zeros((64, LANES), F32)
+        count = jnp.zeros((64, LANES), F32)
+        for line in lines:
+            word = line[:, 8 + h : 9 + h]
+            scale = jnp.exp2(line[:, 126:127].astype(F32))
+            row += jnp.where(lane == 2 * member, decoded(word >> 16, scale), 0.0)
+            row += jnp.where(lane == 2 * member + 1, decoded((word << 16) >> 16, scale), 0.0)
+            count += jnp.where((member == me_ref[0]) & (lane == 10 + h), line, 0).astype(F32)
+        heavy_sums.append(jnp.sum(row, axis=0, keepdims=True))
+        heavy_counts.append(jnp.sum(jnp.sum(count, axis=0, keepdims=True), axis=1, keepdims=True))
+    above, below = [], []
+    for j in range(4):
+        words = [got_ref[pl.ds(t * 320 + j, 64, stride=5), :] for t in range(4)]
+        above.append(sum(decoded(word >> 16, s) for word, s in zip(words, stretch)))
+        below.append(sum(decoded((word << 16) >> 16, s) for word, s in zip(words, stretch)))
+    sums = jnp.concatenate(above + below, axis=0)
+    high = jnp.floor(found * (1.0 / 128.0)) * 128.0
+    low = found - high
+    low = jnp.concatenate([jnp.broadcast_to(low[:, j : j + 1], (64, LANES)) for j in range(8)], axis=0).astype(BF16)
+    high = jnp.concatenate([jnp.broadcast_to(high[:, j : j + 1], (64, LANES)) for j in range(8)], axis=0)
+    high_a, high_b = split2(high)
+    sum_a, sum_b = split2(sums)
+    right = jnp.concatenate([sum_a, sum_b, low, high_a, high_b], axis=1)
+
+    for i in range(4):
         part = slice(i * LANES, (i + 1) * LANES)
-        spot = jnp.broadcast_to(columns[:, i : i + 1], (LANES, 512)).astype(I32)
-        moved = mm(flag(spot == iota((LANES, 512), 1)), right)
+        moved = mm(place_ref[part, :], right)
         total = moved[:, 0:LANES] + moved[:, LANES : 2 * LANES]
         number = moved[:, 2 * LANES : 3 * LANES] + (moved[:, 3 * LANES : 4 * LANES] + moved[:, 4 * LANES :])
         key = iota((LANES, LANES), 0) + i * LANES
         for h in range(2):
             hit = key == heavy_ref[h]
-            spot = 2 * me_ref[0] + h
-            line = own_ref[2:3, :]
-            here = iota((1, LANES), 1)
-            count = jnp.sum(
-                jnp.where(here == spot, line, 0.0) + jnp.where(here == spot + 8, line * 128.0, 0.0), axis=1, keepdims=True
-            )
-            total = jnp.where(hit, own_ref[h : h + 1, :], total)
-            number = jnp.where(hit, count, number)
+            total = jnp.where(hit, heavy_sums[h], total)
+            number = jnp.where(hit, heavy_counts[h], number)
         joined = orders_ref[part, :].astype(F32) * total * lax.rsqrt(1.0 + number)
         joined_s[part, :] = joined
         out_ref[part, :] = joined.astype(BF16)
@@ -446,16 +446,16 @@
     ).astype(BF16)
 
 
-def join(heavy_here, index_y, got, own, slots_here, orders):
+def join(heavy_here, member, got, place, orders):
     vmem = pl.BlockSpec(memory_space=pltpu.VMEM)
     smem = pl.BlockSpec(memory_space=pltpu.SMEM)
     return pl.pallas_call(
         join_kernel,
         out_shape=(jax.ShapeDtypeStruct((512, LANES), BF16), jax.ShapeDtypeStruct((2, LANES), BF16)),
-        in_specs=[smem, smem, vmem, vmem, vmem, vmem],
+        in_specs=[smem, smem, vmem, vmem, vmem],
         scratch_shapes=[pltpu.VMEM((512, LANES), F32)],
         name="join",
-    )(heavy_here, index_y.reshape(1), near(got), near(own), slots_here, orders)
+    )(heavy_here, member.reshape(1), near(got), near(place), orders)
 
 
 def swap(x):
@@ -468,16 +468,16 @@
     owner = ((x * 4 + y) * 2 + low) * 2 + core
     got = swap(pack(row_keys, key_slot, heavy_keys, measures))
     labels = labels_of(owner, key_slot)
-    *sent, kept = owner_sums(t, got, labels)
-    parts = [lax.ppermute(part, "t", [(s, (s + 1 + i) % 4) for s in range(4)]) for i, part in enumerate(sent)]
-    message, own, *rows = quarter_sums(t, parts + [kept], labels)
-    got = swap(message)
-    slot_rows = jnp.where(y == t, rows[0], 0.0)
-    for i in range(1, 4):
-        slot_rows += lax.ppermute(rows[i], ("t", "y"), [(5 * s, 4 * s + (s + i) % 4) for s in range(4)])
+    words, *rows = owner_sums(t, got, labels)
+    got = lax.all_to_all(words.reshape(256, 1, 640), ("t",) + GROUP, split_axis=0, concat_axis=0, tiled=True)
+    got = got.reshape(1280, LANES)
+    slot_rows = sum(
+        lax.ppermute(rows[i], ("t", "y"), [(4 * a + b, 4 * b + (a + i) % 4) for a in range(4) for b in range(4)])
+        for i in range(4)
+    )
     heavy_here = lax.dynamic_slice_in_dim(heavy_keys, device * 2, 2) - device * 512
     slots_here = lax.dynamic_slice_in_dim(key_slot, device * 512, 512).reshape(4, LANES)
-    result, report = join(heavy_here, t, got, own, slots_here, orders)
+    result, report = join(heavy_here, ((x * 2 + low) * 2 + core) * 4 + y, got, places(slots_here), orders)
     return result, report, slot_rows.reshape(512)
 
 

time: 113 us -> 103 us (0.912)
  Pallas kernels: 48.7 us -> 41.5 us
  waiting for transfers between devices: 26.8 us -> 22.7 us
  starting transfers between devices: 32.5 us -> 34.3 us
    all_to_all x0 -> x1, starting transfers between devices: none -> 11 us  [body(): lax.all_to_all(words.reshape(256, 1, 640), ('t',) + GROUP, split_axis=0,...]
    ppermute x6 -> x4, waiting for transfers between devices: 10.8 us -> 3.43 us  [body(): lax.ppermute(rows[i], ('t', 'y'), [(4 * a + b, 4 * b + (a + i) % 4) for a...]
    pallas_call x1, Pallas kernels: 33.7 us -> 27.3 us  [pack(): pl.pallas_call(pack_kernel, out_shape=pltpu.VMEM((64, 80, LANES), I16), i...]
    all_to_all x2 -> x1, starting transfers between devices: 15.8 us -> 10.5 us  [swap(): return lax.all_to_all(x, GROUP, split_axis=0, concat_axis=0, tiled=True)]
    ppermute x6 -> x4, starting transfers between devices: 16.7 us -> 12.8 us  [body(): lax.ppermute(rows[i], ('t', 'y'), [(4 * a + b, 4 * b + (a + i) % 4) for a...]
    all_to_all x0 -> x1, waiting for transfers between devices: none -> 3.33 us  [body(): lax.all_to_all(words.reshape(256, 1, 640), ('t',) + GROUP, split_axis=0,...]
    all_to_all x2 -> x1, waiting for transfers between devices: 16 us -> 16 us  [swap(): return lax.all_to_all(x, GROUP, split_axis=0, concat_axis=0, tiled=True)]
  transfers between devices with their start and end apart: 8 -> 6, of which waited for: 3 -> 3; matrix products, arithmetic and copies ran while one was open for 4% -> 3% of each run, Pallas kernels for 2% -> 4%
where the time goes in v3:
time: 103 us
  Pallas kernels  41.5 us (40%)
  starting transfers between devices  34.3 us (33%)
  waiting for transfers between devices  22.7 us (22%)
  other arithmetic  1.91 us (2%)
  local copies, waits for them, and re-layouts  1.53 us (1%)
    pallas_call x1, Pallas kernels, pack(): pl.pallas_call(pack_kernel, out_shape=pltpu.VMEM((64, 80, LANES), I16), i...  27.3 us
    all_to_all x1, waiting for transfers between devices, swap(): return lax.all_to_all(x, GROUP, split_axis=0, concat_axis=0, tiled=True)  16 us
    ppermute x4, starting transfers between devices, body(): lax.ppermute(rows[i], ('t', 'y'), [(4 * a + b, 4 * b + (a + i) % 4) for a...  12.8 us
    all_to_all x1, starting transfers between devices, body(): lax.all_to_all(words.reshape(256, 1, 640), ('t',) + GROUP, split_axis=0,...  11 us
    all_to_all x1, starting transfers between devices, swap(): return lax.all_to_all(x, GROUP, split_axis=0, concat_axis=0, tiled=True)  10.5 us
    pallas_call x1, Pallas kernels, owner_sums(): pl.pallas_call(owner_kernel, out_shape=(pltpu.VMEM((1280, LANES), I32),)...  7.48 us
    ppermute x4, waiting for transfers between devices, body(): lax.ppermute(rows[i], ('t', 'y'), [(4 * a + b, 4 * b + (a + i) % 4) for a...  3.43 us
    all_to_all x1, waiting for transfers between devices, body(): lax.all_to_all(words.reshape(256, 1, 640), ('t',) + GROUP, split_axis=0,...  3.33 us
  transfers between devices with their start and end apart: 6, of which 3 were waited for; matrix products, arithmetic and copies ran while one was open for 3% of the time, Pallas kernels for 4%

profile of v3, /device:TPU:1, one launch (start us, length us, event | category | flops | bytes accessed | tf_op | source)
XLA Modules:
  0.0 102.7 jit_solution(14977695007043280297)
XLA Ops:
  0.6 27.3 %pack.1 = s16[64,80,128]{2,1,0:T(8,128)(2,1)} custom-call(s32[64,128]{1,0:T(8,128)} %bitcast.20, s32[1024,128]{1,0:T(8,128)} %bitcast.17, s32[4,128]{1,0:T(4,128)} %bitcast.21, bf16[8192,128]{1,0:T(8,128)(2,1)} %rows_hbm.1), custom_call_target="tpu_custom_call" | custom-call | tf_op jit(solution)/shard_map/pack/pallas_call | solution.py:215
  27.9 0.0 copy-start
  27.9 10.5 %all-to-all-start = ((s16[64,80,128]{2,1,0:T(8,128)(2,1)}), s16[64,80,128]{2,1,0:T(8,128)(2,1)S(1)}, u32[]{:S(2)}, u32[]{:S(2)}) async-start(s16[64,80,128]{2,1,0:T(8,128)(2,1)} %pack.1), calls=%async_computation | async-start | bytes 2621440 | tf_op jit(solution)/shard_map/all_to_all | solution.py:462
  38.4 0.0 copy-done
  38.4 0.9 copy.9
  39.3 2.7 %labels.1.label_ref = f32[256,128]{1,0:T(8,128)S(1)} custom-call(s32[1]{0:T(128)} %bitcast.5.me_ref, s32[1024,128]{1,0:T(8,128)} %bitcast.19), custom_call_target="tpu_custom_call" | custom-call | tf_op jit(solution)/shard_map/labels/pallas_call | solution.py:258
  42.0 16.0 %all-to-all-done.got_ref = s16[64,80,128]{2,1,0:T(8,128)(2,1)S(1)} async-done(((s16[64,80,128]{2,1,0:T(8,128)(2,1)}), s16[64,80,128]{2,1,0:T(8,128)(2,1)S(1)}, u32[]{:S(2)}, u32[]{:S(2)}) %all-to-all-start) | async-done | bytes 1310752 | tf_op jit(solution)/shard_map/all_to_all | solution.py:462
  58.0 7.5 %owner.1 = (s32[1280,128]{1,0:T(8,128)}, f32[4,128]{1,0:T(4,128)S(1)}, f32[4,128]{1,0:T(4,128)S(1)}, f32[4,128]{1,0:T(4,128)S(1)}, f32[4,128]{1,0:T(4,128)S(1)}) custom-call(s32[1]{0:T(128)} %bitcast.1.me_ref, s16[64,80,128]{2,1,0:T(8,128)(2,1)S(1)} %all-to-all-done.got_ref, f32[256,128]{1,0:T(8,128)S(1)} %labels.1.label_ref), custom_call_target="tpu_custom_call" | custom-call | tf_op jit(solution)/shard_map/owner/pallas_call | solution.py:367
  65.5 11.0 %all-to-all-start.1 = ((s32[256,1,640]{2,1,0:T(1,128)}), s32[256,1,640]{2,1,0:T(1,128)S(1)}, u32[]{:S(2)}, u32[]{:S(2)}) async-start(s32[256,1,640]{2,1,0:T(1,128)} %bitcast.9), calls=%async_computation.1 | async-start | bytes 1310720 | tf_op jit(solution)/shard_map/all_to_all | solution.py:472
  76.5 0.7 dynamic-slice_bitcast_fusion.slots_ref
  77.2 2.6 %collective-permute-start.3 = (f32[4,128]{1,0:T(4,128)S(1)}, f32[4,128]{1,0:T(4,128)S(1)}, u32[]{:S(2)}, u32[]{:S(2)}) collective-permute-start(f32[4,128]{1,0:T(4,128)S(1)} %get-tuple-element.16), channel_id=1, source_target_pairs={{0,3},{1,19},{2,35},{3,51},{16,0},{17,16},{18,32},{19,48},{32,1},{... | collective-permute-start | bytes 6152 | tf_op jit(solution)/shard_map/ppermute | solution.py:475
  79.8 7.1 %collective-permute-start.2 = (f32[4,128]{1,0:T(4,128)S(1)}, f32[4,128]{1,0:T(4,128)S(1)}, u32[]{:S(2)}, u32[]{:S(2)}) collective-permute-start(f32[4,128]{1,0:T(4,128)S(1)} %get-tuple-element.15), channel_id=1, source_target_pairs={{0,2},{1,18},{2,34},{3,50},{16,3},{17,19},{18,35},{19,51},{32,0},{... | collective-permute-start | bytes 6152 | tf_op jit(solution)/shard_map/ppermute | solution.py:475
  86.8 0.6 collective-permute-start
  87.5 2.4 %collective-permute-start.1 = (f32[4,128]{1,0:T(4,128)S(1)}, f32[4,128]{1,0:T(4,128)S(1)}, u32[]{:S(2)}, u32[]{:S(2)}) collective-permute-start(f32[4,128]{1,0:T(4,128)S(1)} %get-tuple-element.14), channel_id=1, source_target_pairs={{0,1},{1,17},{2,33},{3,49},{16,2},{17,18},{18,34},{19,50},{32,3},{... | collective-permute-start | bytes 6152 | tf_op jit(solution)/shard_map/ppermute | solution.py:475
  89.9 1.3 %dynamic-slice_subtract_fusion.heavy_ref = s32[2]{0:T(128)} fusion(s32[512]{0:T(512)} %param.8, s32[]{:T(128)S(6)} %select_n.6, s32[]{:T(128)S(6)} %mul.40), kind=kLoop, calls=%fused_computation.2 | loop fusion | flops 2 | bytes 24 | tf_op jit(solution)/shard_map/sub | solution.py:478
  91.3 1.2 %places.1.place_ref = bf16[512,512]{1,0:T(8,128)(2,1)S(1)} custom-call(s32[4,128]{1,0:T(4,128)} %dynamic-slice_bitcast_fusion.slots_ref), custom_call_target="tpu_custom_call" | custom-call | tf_op jit(solution)/shard_map/places/pallas_call | solution.py:397
  92.5 0.0 collective-permute-done.3
  92.5 3.4 %collective-permute-done.2 = f32[4,128]{1,0:T(4,128)S(1)} collective-permute-done((f32[4,128]{1,0:T(4,128)S(1)}, f32[4,128]{1,0:T(4,128)S(1)}, u32[]{:S(2)}, u32[]{:S(2)}) %collective-permute-start.2) | collective-permute-done | bytes 2080 | tf_op jit(solution)/shard_map/ppermute | solution.py:475
  95.9 0.0 collective-permute-done
  95.9 0.0 collective-permute-done.1
  95.9 0.6 add_bitcast_fusion
  96.5 3.3 %all-to-all-done.1 = s32[256,1,640]{2,1,0:T(1,128)S(1)} async-done(((s32[256,1,640]{2,1,0:T(1,128)}), s32[256,1,640]{2,1,0:T(1,128)S(1)}, u32[]{:S(2)}, u32[]{:S(2)}) %all-to-all-start.1) | async-done | bytes 655392 | tf_op jit(solution)/shard_map/all_to_all | solution.py:472
  99.8 2.9 %join.1 = (bf16[512,128]{1,0:T(8,128)(2,1)}, bf16[2,128]{1,0:T(2,128)(2,1)}) custom-call(s32[2]{0:T(128)} %dynamic-slice_subtract_fusion.heavy_ref, s32[1]{0:T(128)} %bitcast.me_ref, s32[1280,128]{1,0:T(8,128)S(1)} %bitcast.16, bf16[512,512]{1,0:T(8,128)(2,1)S(1)} %places.1.place_ref, bf16[512,128]{1,0:T(8,128)(2,1)} %orders_ref.1), custom_call_target="tpu_custom_call" | custom-call | tf_op jit(solution)/shard_map/join/pallas_call | solution.py:452
Async XLA Ops:
  27.9 10.5 %copy-start = (s32[131072]{0:T(1024)S(1)}, s32[131072]{0:T(1024)}, u32[]{:S(2)}) copy-start(s32[131072]{0:T(1024)} %param.9) | copy-start | bytes 1572868
  27.9 30.1 %all-to-all-start = ((s16[64,80,128]{2,1,0:T(8,128)(2,1)}), s16[64,80,128]{2,1,0:T(8,128)(2,1)S(1)}, u32[]{:S(2)}, u32[]{:S(2)}) async-start(s16[64,80,128]{2,1,0:T(8,128)(2,1)} %pack.1), calls=%async_computation | async-start | bytes 2621440 | tf_op jit(solution)/shard_map/all_to_all | solution.py:462
  65.5 34.4 %all-to-all-start.1 = ((s32[256,1,640]{2,1,0:T(1,128)}), s32[256,1,640]{2,1,0:T(1,128)S(1)}, u32[]{:S(2)}, u32[]{:S(2)}) async-start(s32[256,1,640]{2,1,0:T(1,128)} %bitcast.9), calls=%async_computation.1 | async-start | bytes 1310720 | tf_op jit(solution)/shard_map/all_to_all | solution.py:472
  77.2 15.3 %collective-permute-start.3 = (f32[4,128]{1,0:T(4,128)S(1)}, f32[4,128]{1,0:T(4,128)S(1)}, u32[]{:S(2)}, u32[]{:S(2)}) collective-permute-start(f32[4,128]{1,0:T(4,128)S(1)} %get-tuple-element.16), channel_id=1, source_target_pairs={{0,3},{1,19},{2,35},{3,51},{16,0},{17,16},{18,32},{19,48},{32,1},{... | collective-permute-start | bytes 6152 | tf_op jit(solution)/shard_map/ppermute | solution.py:475
  79.8 16.1 %collective-permute-start.2 = (f32[4,128]{1,0:T(4,128)S(1)}, f32[4,128]{1,0:T(4,128)S(1)}, u32[]{:S(2)}, u32[]{:S(2)}) collective-permute-start(f32[4,128]{1,0:T(4,128)S(1)} %get-tuple-element.15), channel_id=1, source_target_pairs={{0,2},{1,18},{2,34},{3,50},{16,3},{17,19},{18,35},{19,51},{32,0},{... | collective-permute-start | bytes 6152 | tf_op jit(solution)/shard_map/ppermute | solution.py:475
  86.8 9.1 %collective-permute-start = (f32[4,128]{1,0:T(4,128)S(1)}, f32[4,128]{1,0:T(4,128)S(1)}, u32[]{:S(2)}, u32[]{:S(2)}) collective-permute-start(f32[4,128]{1,0:T(4,128)S(1)} %get-tuple-element.13), channel_id=1, source_target_pairs={{0,0},{1,16},{2,32},{3,48},{16,1},{17,17},{18,33},{19,49},{32,2},{... | collective-permute-start | bytes 6152 | tf_op jit(solution)/shard_map/ppermute | solution.py:475
  87.5 8.4 %collective-permute-start.1 = (f32[4,128]{1,0:T(4,128)S(1)}, f32[4,128]{1,0:T(4,128)S(1)}, u32[]{:S(2)}, u32[]{:S(2)}) collective-permute-start(f32[4,128]{1,0:T(4,128)S(1)} %get-tuple-element.14), channel_id=1, source_target_pairs={{0,1},{1,17},{2,33},{3,49},{16,2},{17,18},{18,34},{19,50},{32,3},{... | collective-permute-start | bytes 6152 | tf_op jit(solution)/shard_map/ppermute | solution.py:475

commit v4 on v3

--- a/solution.py
+++ b/solution.py
@@ -66,6 +66,10 @@
     return s * s * jnp.where(t < 0, -stretch, stretch)
 
 
+def two(a, b):
+    return (a << 16) | (b & 65535)
+
+
 def split2(x):
     high = x.astype(BF16)
     return high, (x - high.astype(F32)).astype(BF16)
@@ -76,7 +80,7 @@
 
 
 def pack_kernel(
-    keys_ref, slots_ref, heavy_ref, rows_hbm, out_ref, rows, table, slot_s, place_s, half_s, count_s, meta_s, masked, sem
+    keys_ref, slots_ref, heavy_ref, rows_hbm, out_ref, rows, table, slot_s, place_s, half_s, count_s, meta_s, masked, sem, word_s
 ):
     row_count = rows.shape[0]
     step = 1024
@@ -105,7 +109,7 @@
         slot_s[:, pl.ds(t * step, step)] = slot
         major = jnp.where(heavy, -1, (slot >> 7) & 511)
         minor = ((slot >> 16) & 1) * LANES + (slot & 127)
-        count_s[...] += mm_nt(hot(512, packed(major)), hot(256, packed(minor)))
+        count_s[...] += mm_nt(hot(512, packed(major)).astype(jnp.float8_e4m3fn), hot(256, packed(minor)).astype(jnp.float8_e4m3fn))
         return carry
 
     lax.fori_loop(0, steps, look_up, 0, unroll=8)
@@ -197,24 +201,28 @@
     def light_block(b, carry):
         total = coded(block_sums(b, 512), shrink_light)
         for h in range(2):
-            piece = total[:, h * LANES : (h + 1) * LANES].astype(I32).astype(I16).reshape(8, 64, LANES)
-            out_ref[pl.ds(h * 32 + b * 8, 8), 0:64, :] = piece
+            piece = total[:, h * LANES : (h + 1) * LANES].astype(I32).reshape(8, 64, LANES)
+            words = two(piece[:, :32], piece[:, 32:])
+            for i in range(8):
+                out_ref[pl.ds((h * 32 + b * 8 + i) * 37, 32), :] = words[i]
         return carry
 
     lax.fori_loop(0, 4, light_block, 0, unroll=2)
     total = coded(block_sums(jnp.int32(8), 256), shrink_heavy)
-    turned = jnp.concatenate([total[:, :LANES].T, total[:, LANES:].T], axis=1)
-    sums = jnp.concatenate([turned[:, k * LANES : (k + 1) * LANES].reshape(64, 2, LANES) for k in range(4)], axis=1)
-    sub = iota((64, 8, LANES), 1)
-    extra = jnp.where(sub == 0, first[:, None, :], jnp.where(sub == 1, second[:, None, :], 0.0))
-    out_ref[:, 64:80, :] = jnp.concatenate([sums, extra], axis=1).astype(I32).astype(I16)
+    turned = jnp.concatenate([total[:, :LANES].T, total[:, LANES:].T], axis=1).astype(I32)
+    for k in range(2):
+        word_s[...] = two(turned[:, k * LANES : (k + 1) * LANES], turned[:, (k + 2) * LANES : (k + 3) * LANES])
+        for c in range(2):
+            out_ref[pl.ds(32 + 2 * k + c, 64, stride=37), :] = word_s[pl.ds(c, 64, stride=2), :]
+    words = two(first.astype(I32), pltpu.roll(first, 64, 1).astype(I32))
+    out_ref[pl.ds(36, 64, stride=37), :] = jnp.where(lane < 64, words, pltpu.roll(second, 64, 1).astype(I32))
 
 
 def pack(row_keys, key_slot, heavy_keys, measures):
     n = measures.shape[0]
     return pl.pallas_call(
         pack_kernel,
-        out_shape=pltpu.VMEM((64, 80, LANES), I16),
+        out_shape=pltpu.VMEM((2368, LANES), I32),
         in_specs=[pl.BlockSpec(memory_space=pltpu.VMEM)] * 3 + [pl.BlockSpec(memory_space=pl.ANY)],
         scratch_shapes=[
             pltpu.VMEM((n, LANES), BF16),
@@ -226,6 +234,7 @@
             pltpu.VMEM((208, LANES), F32),
             pltpu.VMEM((n, 256), BF16),
             pltpu.SemaphoreType.DMA,
+            pltpu.VMEM((LANES, LANES), I32),
         ],
         compiler_params=pltpu.CompilerParams(vmem_limit_bytes=56 * 2**20),
         name="pack",
@@ -280,12 +289,15 @@
 
 
 def owner_kernel(me_ref, got_ref, label_ref, out_ref, r0_ref, r1_ref, r2_ref, r3_ref, pair_s, index_s, weight_s):
-    sources = got_ref.shape[0]
-    tail = got_ref[:, 64:80, :].astype(F32)
-    first = tail[:, 8, :]
-    second = tail[:, 9, :]
-    stretch = jnp.exp2(tail[:, 9:10, LANES - 1 :] + 8.0)
-    heavy = jnp.sum(decoded(tail[:, 0:8, :], stretch * 32.0), axis=0)
+    sources = 64
+    meta = got_ref[pl.ds(36, 64, stride=37), :]
+    second = pltpu.roll(meta, 64, 1).astype(F32)
+    counts = (meta & 65535).astype(F32)
+    first = jnp.where(iota((64, LANES), 1) < 64, (meta >> 16).astype(F32), pltpu.roll(counts, 64, 1))
+    stretch = jnp.exp2(meta[:, LANES - 1 :].astype(F32) + 8.0)
+    heavy = [got_ref[pl.ds(32 + r, 64, stride=37), :] for r in range(4)]
+    heavy = [decoded(word >> 16, stretch * 32.0) for word in heavy] + [decoded((word << 16) >> 16, stretch * 32.0) for word in heavy]
+    heavy = jnp.concatenate([jnp.sum(part, axis=0, keepdims=True) for part in heavy], axis=0)
     heavy_counts = jnp.sum(second, axis=0, keepdims=True)
 
     swapped = pltpu.roll(first, 64, 1)
@@ -298,11 +310,14 @@
         weight = jnp.where(low_lane, swapped[even], first[odd])
         weight_s[:, at] = jnp.broadcast_to(weight, (16, LANES)).astype(BF16)
 
-    for s in range(0, sources, 8):
-        values = decoded(got_ref[s : s + 8, 0:64, :].astype(I32), stretch[s : s + 8]).reshape(512, LANES)
-        high, low = split2(values)
-        pair_s[s * 64 : (s + 8) * 64, 0:LANES] = high
-        pair_s[s * 64 : (s + 8) * 64, LANES:] = low
+    for s in range(sources):
+        word = got_ref[s * 37 : s * 37 + 32, :]
+        scale = stretch[s : s + 1]
+        for i, code in enumerate((word >> 16, (word << 16) >> 16)):
+            high, low = split2(decoded(code, scale))
+            at = slice(s * 64 + i * 32, s * 64 + i * 32 + 32)
+            pair_s[at, 0:LANES] = high
+            pair_s[at, LANES:] = low
 
     wide = index_s[...].astype(I32)[0:8]
     histogram = mm_nt(hot(16, packed(wide >> 7)) * weight_s[...], hot(LANES, packed(wide & 127)))
@@ -466,7 +481,7 @@
     x, t, low, core, y = (lax.axis_index(name) for name in AXES)
     device = (((x * 4 + t) * 2 + low) * 2 + core) * 4 + y
     owner = ((x * 4 + y) * 2 + low) * 2 + core
-    got = swap(pack(row_keys, key_slot, heavy_keys, measures))
+    got = swap(pack(row_keys, key_slot, heavy_keys, measures).reshape(64, 1, -1)).reshape(-1, LANES)
     labels = labels_of(owner, key_slot)
     words, *rows = owner_sums(t, got, labels)
     got = lax.all_to_all(words.reshape(256, 1, 640), ("t",) + GROUP, split_axis=0, concat_axis=0, tiled=True)

time: 103 us -> 101 us (0.981)
  no operation moved by 1% of the time
where the time goes in v4:
time: 101 us
  Pallas kernels  40.5 us (40%)
  starting transfers between devices  34.2 us (34%)
  waiting for transfers between devices  21.8 us (22%)
  other arithmetic  1.91 us (2%)
  local copies, waits for them, and re-layouts  1.52 us (2%)
    pallas_call x1, Pallas kernels, pack(): pl.pallas_call(pack_kernel, out_shape=pltpu.VMEM((2368, LANES), I32), in_...  26.4 us
    all_to_all x1, waiting for transfers between devices, swap(): return lax.all_to_all(x, GROUP, split_axis=0, concat_axis=0, tiled=True)  15 us
    ppermute x4, starting transfers between devices, body(): lax.ppermute(rows[i], ('t', 'y'), [(4 * a + b, 4 * b + (a + i) % 4) for a...  12.8 us
    all_to_all x1, starting transfers between devices, body(): lax.all_to_all(words.reshape(256, 1, 640), ('t',) + GROUP, split_axis=0,...  11 us
    all_to_all x1, starting transfers between devices, swap(): return lax.all_to_all(x, GROUP, split_axis=0, concat_axis=0, tiled=True)  10.5 us
    pallas_call x1, Pallas kernels, owner_sums(): pl.pallas_call(owner_kernel, out_shape=(pltpu.VMEM((1280, LANES), I32),)...  7.27 us
    ppermute x4, waiting for transfers between devices, body(): lax.ppermute(rows[i], ('t', 'y'), [(4 * a + b, 4 * b + (a + i) % 4) for a...  3.43 us
    all_to_all x1, waiting for transfers between devices, body(): lax.all_to_all(words.reshape(256, 1, 640), ('t',) + GROUP, split_axis=0,...  3.33 us
  transfers between devices with their start and end apart: 6, of which 3 were waited for; matrix products, arithmetic and copies ran while one was open for 3% of the time, Pallas kernels for 4%

profile of v4, /device:TPU:1, one launch (start us, length us, event | category | flops | bytes accessed | tf_op | source)
XLA Modules:
  0.0 100.6 jit_solution(1371354539417048814)
XLA Ops:
  0.6 26.4 %pack.1 = s32[2368,128]{1,0:T(8,128)} custom-call(s32[64,128]{1,0:T(8,128)} %bitcast.23, s32[1024,128]{1,0:T(8,128)} %bitcast.20, s32[4,128]{1,0:T(4,128)} %bitcast.24, bf16[8192,128]{1,0:T(8,128)(2,1)} %rows_hbm.1), custom_call_target="tpu_custom_call" | custom-call | tf_op jit(solution)/shard_map/pack/pallas_call | solution.py:223
  27.1 0.0 copy-start
  27.1 10.5 %all-to-all-start = ((s32[64,1,4736]{2,1,0:T(1,128)}), s32[64,1,4736]{2,1,0:T(1,128)S(1)}, u32[]{:S(2)}, u32[]{:S(2)}) async-start(s32[64,1,4736]{2,1,0:T(1,128)} %bitcast.5), calls=%async_computation | async-start | bytes 2424832 | tf_op jit(solution)/shard_map/all_to_all | solution.py:477
  37.6 0.0 copy-done
  37.6 0.9 copy.10
  38.4 2.7 %labels.1.label_ref = f32[256,128]{1,0:T(8,128)S(1)} custom-call(s32[1]{0:T(128)} %bitcast.7.me_ref, s32[1024,128]{1,0:T(8,128)} %bitcast.22), custom_call_target="tpu_custom_call" | custom-call | tf_op jit(solution)/shard_map/labels/pallas_call | solution.py:267
  41.1 15.0 %all-to-all-done = s32[64,1,4736]{2,1,0:T(1,128)S(1)} async-done(((s32[64,1,4736]{2,1,0:T(1,128)}), s32[64,1,4736]{2,1,0:T(1,128)S(1)}, u32[]{:S(2)}, u32[]{:S(2)}) %all-to-all-start) | async-done | bytes 1212448 | tf_op jit(solution)/shard_map/all_to_all | solution.py:477
  56.1 7.3 %owner.1 = (s32[1280,128]{1,0:T(8,128)}, f32[4,128]{1,0:T(4,128)S(1)}, f32[4,128]{1,0:T(4,128)S(1)}, f32[4,128]{1,0:T(4,128)S(1)}, f32[4,128]{1,0:T(4,128)S(1)}) custom-call(s32[1]{0:T(128)} %bitcast.1.me_ref, s32[2368,128]{1,0:T(8,128)S(1)} %bitcast.18, f32[256,128]{1,0:T(8,128)S(1)} %labels.1.label_ref), custom_call_target="tpu_custom_call" | custom-call | tf_op jit(solution)/shard_map/owner/pallas_call | solution.py:382
  63.4 11.0 %all-to-all-start.1 = ((s32[256,1,640]{2,1,0:T(1,128)}), s32[256,1,640]{2,1,0:T(1,128)S(1)}, u32[]{:S(2)}, u32[]{:S(2)}) async-start(s32[256,1,640]{2,1,0:T(1,128)} %bitcast.11), calls=%async_computation.1 | async-start | bytes 1310720 | tf_op jit(solution)/shard_map/all_to_all | solution.py:487
  74.4 0.7 dynamic-slice_bitcast_fusion.slots_ref
  75.0 2.6 %collective-permute-start.3 = (f32[4,128]{1,0:T(4,128)S(1)}, f32[4,128]{1,0:T(4,128)S(1)}, u32[]{:S(2)}, u32[]{:S(2)}) collective-permute-start(f32[4,128]{1,0:T(4,128)S(1)} %get-tuple-element.16), channel_id=1, source_target_pairs={{0,3},{1,19},{2,35},{3,51},{16,0},{17,16},{18,32},{19,48},{32,1},{... | collective-permute-start | bytes 6152 | tf_op jit(solution)/shard_map/ppermute | solution.py:490
  77.7 7.1 %collective-permute-start.2 = (f32[4,128]{1,0:T(4,128)S(1)}, f32[4,128]{1,0:T(4,128)S(1)}, u32[]{:S(2)}, u32[]{:S(2)}) collective-permute-start(f32[4,128]{1,0:T(4,128)S(1)} %get-tuple-element.15), channel_id=1, source_target_pairs={{0,2},{1,18},{2,34},{3,50},{16,3},{17,19},{18,35},{19,51},{32,0},{... | collective-permute-start | bytes 6152 | tf_op jit(solution)/shard_map/ppermute | solution.py:490
  84.7 0.6 collective-permute-start
  85.4 2.4 %collective-permute-start.1 = (f32[4,128]{1,0:T(4,128)S(1)}, f32[4,128]{1,0:T(4,128)S(1)}, u32[]{:S(2)}, u32[]{:S(2)}) collective-permute-start(f32[4,128]{1,0:T(4,128)S(1)} %get-tuple-element.14), channel_id=1, source_target_pairs={{0,1},{1,17},{2,33},{3,49},{16,2},{17,18},{18,34},{19,50},{32,3},{... | collective-permute-start | bytes 6152 | tf_op jit(solution)/shard_map/ppermute | solution.py:490
  87.8 1.3 %dynamic-slice_subtract_fusion.heavy_ref = s32[2]{0:T(128)} fusion(s32[512]{0:T(512)} %param.8, s32[]{:T(128)S(6)} %select_n.6, s32[]{:T(128)S(6)} %mul.40), kind=kLoop, calls=%fused_computation.2 | loop fusion | flops 2 | bytes 24 | tf_op jit(solution)/shard_map/sub | solution.py:493
  89.1 1.2 %places.1.place_ref = bf16[512,512]{1,0:T(8,128)(2,1)S(1)} custom-call(s32[4,128]{1,0:T(4,128)} %dynamic-slice_bitcast_fusion.slots_ref), custom_call_target="tpu_custom_call" | custom-call | tf_op jit(solution)/shard_map/places/pallas_call | solution.py:412
  90.4 0.0 collective-permute-done.3
  90.4 3.4 %collective-permute-done.2 = f32[4,128]{1,0:T(4,128)S(1)} collective-permute-done((f32[4,128]{1,0:T(4,128)S(1)}, f32[4,128]{1,0:T(4,128)S(1)}, u32[]{:S(2)}, u32[]{:S(2)}) %collective-permute-start.2) | collective-permute-done | bytes 2080 | tf_op jit(solution)/shard_map/ppermute | solution.py:490
  93.8 0.0 collective-permute-done
  93.8 0.0 collective-permute-done.1
  93.8 0.6 add_bitcast_fusion
  94.4 3.3 %all-to-all-done.1 = s32[256,1,640]{2,1,0:T(1,128)S(1)} async-done(((s32[256,1,640]{2,1,0:T(1,128)}), s32[256,1,640]{2,1,0:T(1,128)S(1)}, u32[]{:S(2)}, u32[]{:S(2)}) %all-to-all-start.1) | async-done | bytes 655392 | tf_op jit(solution)/shard_map/all_to_all | solution.py:487
  97.7 2.9 %join.1 = (bf16[512,128]{1,0:T(8,128)(2,1)}, bf16[2,128]{1,0:T(2,128)(2,1)}) custom-call(s32[2]{0:T(128)} %dynamic-slice_subtract_fusion.heavy_ref, s32[1]{0:T(128)} %bitcast.me_ref, s32[1280,128]{1,0:T(8,128)S(1)} %bitcast.19, bf16[512,512]{1,0:T(8,128)(2,1)S(1)} %places.1.place_ref, bf16[512,128]{1,0:T(8,128)(2,1)} %orders_ref.1), custom_call_target="tpu_custom_call" | custom-call | tf_op jit(solution)/shard_map/join/pallas_call | solution.py:467
Async XLA Ops:
  27.1 10.5 %copy-start = (s32[131072]{0:T(1024)S(1)}, s32[131072]{0:T(1024)}, u32[]{:S(2)}) copy-start(s32[131072]{0:T(1024)} %param.9) | copy-start | bytes 1572868
  27.1 29.1 %all-to-all-start = ((s32[64,1,4736]{2,1,0:T(1,128)}), s32[64,1,4736]{2,1,0:T(1,128)S(1)}, u32[]{:S(2)}, u32[]{:S(2)}) async-start(s32[64,1,4736]{2,1,0:T(1,128)} %bitcast.5), calls=%async_computation | async-start | bytes 2424832 | tf_op jit(solution)/shard_map/all_to_all | solution.py:477
  63.4 34.3 %all-to-all-start.1 = ((s32[256,1,640]{2,1,0:T(1,128)}), s32[256,1,640]{2,1,0:T(1,128)S(1)}, u32[]{:S(2)}, u32[]{:S(2)}) async-start(s32[256,1,640]{2,1,0:T(1,128)} %bitcast.11), calls=%async_computation.1 | async-start | bytes 1310720 | tf_op jit(solution)/shard_map/all_to_all | solution.py:487
  75.0 15.3 %collective-permute-start.3 = (f32[4,128]{1,0:T(4,128)S(1)}, f32[4,128]{1,0:T(4,128)S(1)}, u32[]{:S(2)}, u32[]{:S(2)}) collective-permute-start(f32[4,128]{1,0:T(4,128)S(1)} %get-tuple-element.16), channel_id=1, source_target_pairs={{0,3},{1,19},{2,35},{3,51},{16,0},{17,16},{18,32},{19,48},{32,1},{... | collective-permute-start | bytes 6152 | tf_op jit(solution)/shard_map/ppermute | solution.py:490
  77.7 16.1 %collective-permute-start.2 = (f32[4,128]{1,0:T(4,128)S(1)}, f32[4,128]{1,0:T(4,128)S(1)}, u32[]{:S(2)}, u32[]{:S(2)}) collective-permute-start(f32[4,128]{1,0:T(4,128)S(1)} %get-tuple-element.15), channel_id=1, source_target_pairs={{0,2},{1,18},{2,34},{3,50},{16,3},{17,19},{18,35},{19,51},{32,0},{... | collective-permute-start | bytes 6152 | tf_op jit(solution)/shard_map/ppermute | solution.py:490
  84.7 9.1 %collective-permute-start = (f32[4,128]{1,0:T(4,128)S(1)}, f32[4,128]{1,0:T(4,128)S(1)}, u32[]{:S(2)}, u32[]{:S(2)}) collective-permute-start(f32[4,128]{1,0:T(4,128)S(1)} %get-tuple-element.13), channel_id=1, source_target_pairs={{0,0},{1,16},{2,32},{3,48},{16,1},{17,17},{18,33},{19,49},{32,2},{... | collective-permute-start | bytes 6152 | tf_op jit(solution)/shard_map/ppermute | solution.py:490
  85.4 8.4 %collective-permute-start.1 = (f32[4,128]{1,0:T(4,128)S(1)}, f32[4,128]{1,0:T(4,128)S(1)}, u32[]{:S(2)}, u32[]{:S(2)}) collective-permute-start(f32[4,128]{1,0:T(4,128)S(1)} %get-tuple-element.14), channel_id=1, source_target_pairs={{0,1},{1,17},{2,33},{3,49},{16,2},{17,18},{18,34},{19,50},{32,3},{... | collective-permute-start | bytes 6152 | tf_op jit(solution)/shard_map/ppermute | solution.py:490
